TPU v7x, 32 devices: a whole 2x2x4 slice. The times are simulated.
32 devices in a mesh: gy: 16 (over z, x, core), gz: 2 (over y).
Axes of the slice: x: 2, y: 2, z: 4, core: 2. Of those that a mesh axis runs over, the one named last changes fastest.
Arguments:
- populations: float32 [19, 4, 128, 2048], P(None, None, 'gy', 'gz'), may hold values from 0 to 1, as said below
- solid_mask: int32 [4, 128, 2048], P(None, 'gy', 'gz'), may hold values 0 or 1
- body_force: float32 [3], replicated, may hold values from 0.002 to 0.008
Outputs:
- density: float32 [4, 128, 2048], P(None, 'gy', 'gz')
- velocity: float32 [3, 4, 128, 2048], P(None, None, 'gy', 'gz')
Inputs may be any that keep to these rules, and one draw needn't show every extreme that they name: `populations`: every population is positive, near its lattice weight times one.
All inputs are finite; a program needn't handle non-finite values. No bound on the sum of `solid_mask` on one device may be relied on, other than what follows from the above.
Results may differ from a plain program's by a relative error of at most 0.0003.
Values sent between devices are 32-bit elements; how exact they have to be, the bound alone decides.
A program may use at most 64 MiB of HBM per device.

v0:
```python
import functools

import jax
import jax.numpy as jnp
from jax import lax
from jax.experimental import pallas as pl
from jax.experimental.pallas import tpu as pltpu
from jax.sharding import PartitionSpec as P

STEPS = 3
W = 128
UNROLL = 8
VMEM_LIMIT = 24 << 20

velocities = [
    (0, 0, 0),
    (1, 0, 0),
    (-1, 0, 0),
    (0, 1, 0),
    (0, -1, 0),
    (0, 0, 1),
    (0, 0, -1),
    (1, 1, 0),
    (-1, -1, 0),
    (1, -1, 0),
    (-1, 1, 0),
    (1, 0, 1),
    (-1, 0, -1),
    (1, 0, -1),
    (-1, 0, 1),
    (0, 1, 1),
    (0, -1, -1),
    (0, 1, -1),
    (0, -1, 1),
]
opposite = [0, 2, 1, 4, 3, 6, 5, 8, 7, 10, 9, 12, 11, 14, 13, 16, 15, 18, 17]
reference_mach = 0.05
Y_SET = {s: [k for k in range(19) if velocities[k][1] == s] for s in (1, -1)}
Z_SET = {s: [k for k in range(19) if velocities[k][2] == s] for s in (1, -1)}
ROUTES = [(1, 0), (-1, 0), (0, 1), (0, -1), (1, 1), (-1, 1), (1, -1), (-1, -1)]


def moments(f):
    s = [f[2 * a + 1] + f[2 * a + 2] for a in range(9)]
    d = [f[2 * a + 1] - f[2 * a + 2] for a in range(9)]
    axy, axz, ayz = s[3] + s[4], s[5] + s[6], s[7] + s[8]
    bxy, bxz, byz = s[3] - s[4], s[5] - s[6], s[7] - s[8]
    pxy, pxz, pyz = d[3] + d[4], d[5] + d[6], d[7] + d[8]
    qxy, qxz, qyz = d[3] - d[4], d[5] - d[6], d[7] - d[8]
    rho = (f[0] + s[0]) + (s[1] + s[2]) + ((axy + axz) + ayz)
    jx = d[0] + (pxy + pxz)
    jy = d[1] + (qxy + pyz)
    jz = d[2] + (qxz + qyz)
    return s, (axy, axz, ayz), (bxy, bxz, byz), (pxy, pxz, pyz), (qxy, qxz, qyz), rho, jx, jy, jz


def collide(f, force):
    s, (axy, axz, ayz), (bxy, bxz, byz), (pxy, pxz, pyz), (qxy, qxz, qyz), rho, jx, jy, jz = moments(f)
    inv = 1.0 / rho
    ux, uy, uz = jx * inv, jy * inv, jz * inv
    rxx, ryy, rzz = jx * ux, jy * uy, jz * uz
    third, ninth = rho * (1.0 / 3.0), rho * (1.0 / 9.0)
    e = 0.625
    exx = e * (s[0] + axy + axz - third - rxx)
    eyy = e * (s[1] + axy + ayz - third - ryy)
    ezz = e * (s[2] + axz + ayz - third - rzz)
    gxy = 0.5 * e * (bxy - jx * uy)
    gxz = 0.5 * e * (bxz - jx * uz)
    gyz = 0.5 * e * (byz - jy * uz)
    sq = (rxx + ryy + rzz) * (1.0 / 3.0)
    h = 0.65
    base = ninth + sq
    hxy = h * (axy - base + 0.5 * rzz)
    hxz = h * (axz - base + 0.5 * ryy)
    hyz = h * (ayz - base + 0.5 * rxx)
    t = 0.8
    jx3, jy3, jz3 = jx * (1.0 / 3.0), jy * (1.0 / 3.0), jz * (1.0 / 3.0)
    tpxy, tpxz, tpyz = t * (pxy - jx3), t * (pxz - jx3), t * (pyz - jy3)
    tqxy, tqxz, tqyz = t * (qxy - jy3), t * (qxz - jz3), t * (qyz - jz3)
    fx, fy, fz = force
    axis_w, edge_w = 3.0 / 18.0, 3.0 / 36.0
    even = [exx - hxy - hxz, eyy - hxy - hyz, ezz - hxz - hyz]
    odd = [-(tpxy + tpxz) - axis_w * fx, -(tqxy + tpyz) - axis_w * fy, -(tqxz + tqyz) - axis_w * fz]
    edges = (
        (hxy, gxy, tpxy, tqxy, fx, fy),
        (hxz, gxz, tpxz, tqxz, fx, fz),
        (hyz, gyz, tpyz, tqyz, fy, fz),
    )
    for hh, gg, tp, tq, fa, fb in edges:
        even += [0.5 * hh + gg, 0.5 * hh - gg]
        odd += [0.5 * (tp + tq) - edge_w * (fa + fb), 0.5 * (tp - tq) - edge_w * (fa - fb)]
    out = [f[0] + 2.0 * ((exx + eyy + ezz) - (hxy + hxz + hyz))]
    for a in range(9):
        out.append(f[2 * a + 1] - even[a] - odd[a])
        out.append(f[2 * a + 2] - even[a] + odd[a])
    return out


def kernel(gy, gz, pop_hbm, mask_hbm, force_ref, out_ref, raw, mask, bits, cells, ys, yh, zs, zh,
           mys, myh, mzs, mzh, load_sem, send_sem, recv_sem):
    planes, across, length = mask_hbm.shape
    chunks = length // W
    my, mz = lax.axis_index("gy"), lax.axis_index("gz")

    def peer(dy, dz):
        return {"gy": lax.rem(my + dy + gy, gy), "gz": lax.rem(mz + dz + gz, gz)}

    load_mask = pltpu.make_async_copy(mask_hbm, mask.at[:, :, W : W + length], load_sem.at[0])
    load_pop = [pltpu.make_async_copy(pop_hbm.at[:, p], raw.at[p], load_sem.at[1 + p]) for p in range(planes)]
    load_mask.start()
    for copy in load_pop:
        copy.start()
    barrier = pltpu.get_barrier_semaphore()
    for dy, dz in ROUTES:
        pl.semaphore_signal(barrier, inc=1, device_id=peer(dy, dz), device_id_type=pl.DeviceIdType.MESH)

    lane = lax.broadcasted_iota(jnp.int32, (across, W), 1)
    sub = lax.broadcasted_iota(jnp.int32, (across, W), 0)
    edge_row = {1: across - 1, -1: 0}

    def copies(number, rows_out, rows_in, packed_out, packed_in):
        result = []
        for i, (dy, dz) in enumerate(ROUTES):
            if dz == 0:
                side = (1 - dy) // 2
                source, target = rows_out.at[side], rows_in.at[side, :, W : W + length]
            else:
                source, target = packed_out.at[(1 - dz) // 2], packed_in.at[i - 2]
            result.append(
                pltpu.make_async_remote_copy(
                    src_ref=source,
                    dst_ref=target,
                    send_sem=send_sem.at[number, i],
                    recv_sem=recv_sem.at[number, i],
                    device_id=peer(dy, dz),
                    device_id_type=pl.DeviceIdType.MESH,
                )
            )
        return result

    def pack_columns(items, first, zero):
        packed = zero
        for j, block in enumerate(items):
            shift = (j if first else j + 1) % W
            moved = pltpu.roll(block, shift, 1) if shift else block
            packed = jnp.where(lane == j, moved, packed)
        return packed

    def unpack(block, j, last):
        shift = (W - 1 - j if last else W - j) % W
        return pltpu.roll(block, shift, 1) if shift else block

    def pull(cell, row, c, base):
        cy, cz = c[1], c[2]

        def at(offset):
            v = cell(offset)
            if cy:
                v = jnp.where(sub == edge_row[cy], row(offset), v)
            return v

        v = at(base)
        if cz == 1:
            v = pltpu.roll(jnp.where(lane == W - 1, at(base - W), v), 1, 1)
        elif cz == -1:
            v = pltpu.roll(jnp.where(lane == 0, at(base + W), v), W - 1, 1)
        if cy:
            v = pltpu.roll(v, 1 if cy == 1 else across - 1, 0)
        return v

    load_mask.wait()
    for side, sign in enumerate((1, -1)):
        for p in range(planes):
            r = edge_row[sign]
            mys[side, p : p + 1, :] = mask[p, r : r + 1, W : W + length]
        offset = length if sign == 1 else W
        mzs[side] = pack_columns(
            [mask[p, :, offset : offset + W] for p in range(planes)], sign == -1, jnp.zeros((across, W), jnp.int32)
        )
    pl.semaphore_wait(barrier, len(ROUTES))
    mask_copies = copies(0, mys, myh, mzs, mzh)
    for copy in mask_copies:
        copy.start()

    force = (force_ref[0], force_ref[1], force_ref[2])

    def relax_and_store(step, f, p, base, into):
        relaxed = collide(f, force)
        for k in range(19):
            cells[into, k, p, :, pl.ds(base, W)] = relaxed[k]
        start = pl.multiple_of(base - W, W)
        for side, sign in enumerate((1, -1)):
            r = edge_row[sign]
            for i, k in enumerate(Y_SET[sign]):
                ys[step, p, side, i : i + 1, pl.ds(start, W)] = relaxed[k][r : r + 1, :]

    def send(step, into, p):
        for side, sign in enumerate((1, -1)):
            offset = length if sign == 1 else W
            zs[step, p, side] = pack_columns(
                [cells[into, k, p, :, offset : offset + W] for k in Z_SET[sign]],
                sign == -1,
                jnp.zeros((across, W), jnp.float32),
            )
        out = copies(1 + step * planes + p, ys.at[step, p], yh.at[step, p], zs.at[step, p], zh.at[step, p])
        for copy in out:
            copy.start()
        return out

    def arrive(step, into, out, p):
        for copy in out:
            copy.wait_recv()
        for zsign in (1, -1):
            offset = 0 if zsign == 1 else W + length
            block = zh[step, p, ROUTES.index((0, zsign)) - 2]
            for i, k in enumerate(Z_SET[zsign]):
                cells[into, k, p, :, offset : offset + W] = unpack(block, i, zsign == 1)
            for yside, ysign in enumerate((1, -1)):
                corner = zh[step, p, ROUTES.index((ysign, zsign)) - 2]
                r = edge_row[ysign]
                k = velocities.index((0, ysign, zsign))
                moved = unpack(corner, Z_SET[zsign].index(k), zsign == 1)
                j = Y_SET[ysign].index(k)
                yh[step, p, yside, j : j + 1, offset : offset + W] = moved[r : r + 1, :]

    def streamed(step, into, p, base):
        flags = bits[p, :, pl.ds(pl.multiple_of(base - W, W), W)]
        f = []
        for k in range(19):
            c = velocities[k]
            here = cells[into, opposite[k], p, :, pl.ds(base, W)]
            q = p - c[0]
            if k == 0:
                moved = here
            elif q < 0 or q >= planes:
                f.append(here)
                continue
            else:

                def cell(offset, k=k, q=q):
                    return cells[into, k, q, :, pl.ds(pl.multiple_of(offset, W), W)]

                def row(offset, k=k, q=q, c=c):
                    j = Y_SET[c[1]].index(k)
                    return yh[step, q, (1 - c[1]) // 2, j : j + 1, pl.ds(pl.multiple_of(offset, W), W)]

                moved = pull(cell, row, c, base)
            f.append(moved if k == 0 else jnp.where((flags & (1 << k)) != 0, here, moved))
        return f

    unroll = max(u for u in (UNROLL, 4, 2, 1) if chunks % u == 0)

    def over_chunks(block):
        def group(i, carry):
            for n in range(unroll):
                block(pl.multiple_of((i * unroll + (n + 1)) * W, W))
            return carry

        lax.fori_loop(0, chunks // unroll, group, 0)

    flying = []
    for p in range(planes):
        load_pop[p].wait()

        def first(base, p=p):
            f = [raw[p, k, :, pl.ds(pl.multiple_of(base - W, W), W)] for k in range(19)]
            relax_and_store(0, f, p, base, 0)

        over_chunks(first)
        flying.append(send(0, 0, p))

    for copy in mask_copies:
        copy.wait_recv()
    for zside, zsign in enumerate((1, -1)):
        offset = 0 if zsign == 1 else W + length
        block = mzh[ROUTES.index((0, zsign)) - 2]
        for p in range(planes):
            mask[p, :, offset : offset + W] = unpack(block, p, zsign == 1)
        for yside, ysign in enumerate((1, -1)):
            corner = mzh[ROUTES.index((ysign, zsign)) - 2]
            r = edge_row[ysign]
            for p in range(planes):
                moved = unpack(corner, p, zsign == 1)
                myh[yside, p : p + 1, offset : offset + W] = moved[r : r + 1, :]

    def flag(i, carry):
        base = pl.multiple_of((i + 1) * W, W)
        shifted = {}
        for q in range(planes):

            def cell(offset, q=q):
                return mask[q, :, pl.ds(pl.multiple_of(offset, W), W)]

            for cy in (0, 1, -1):

                def row(offset, q=q, cy=cy):
                    return myh[(1 - cy) // 2, q : q + 1, pl.ds(pl.multiple_of(offset, W), W)]

                for cz in (0, 1, -1):
                    shifted[q, cy, cz] = pull(cell, row, (0, cy, cz), base)
        for p in range(planes):
            word = jnp.zeros((across, W), jnp.int32)
            for k in range(1, 19):
                c = velocities[k]
                q = p - c[0]
                if 0 <= q < planes:
                    word = word | jnp.where(shifted[q, c[1], c[2]] > 0, 1 << k, 0)
            bits[p, :, pl.ds(pl.multiple_of(base - W, W), W)] = word
        return carry

    lax.fori_loop(0, chunks, flag, 0)

    all_copies = [mask_copies] + flying
    for step in range(STEPS):
        source, into = step % 2, (step + 1) % 2
        started = []
        arrived = 0
        for p in range(planes):
            while arrived < min(p + 2, planes):
                arrive(step, source, flying[arrived], arrived)
                arrived += 1

            def middle(base, p=p, step=step, source=source, into=into):
                relax_and_store(step + 1, streamed(step, source, p, base), p, base, into)

            def final(base, p=p, step=step, source=source):
                spot = pl.ds(pl.multiple_of(base - W, W), W)
                rho, jx, jy, jz = moments(streamed(step, source, p, base))[-4:]
                fluid = (1 - mask[p, :, pl.ds(base, W)]).astype(jnp.float32)
                scale = fluid * (1.0 / reference_mach) / rho
                out_ref[0, p, :, spot] = rho * fluid
                out_ref[1, p, :, spot] = jx * scale
                out_ref[2, p, :, spot] = jy * scale
                out_ref[3, p, :, spot] = jz * scale

            if step < STEPS - 1:
                over_chunks(middle)
                started.append(send(step + 1, into, p))
            else:
                over_chunks(final)
        flying = started
        all_copies += flying
    for group in all_copies:
        for copy in group:
            copy.wait_send()


def hand_out(both_ref, den_hbm, vel_hbm, sem):
    den = pltpu.make_async_copy(both_ref.at[0], den_hbm, sem.at[0])
    vel = pltpu.make_async_copy(both_ref.at[pl.ds(1, 3)], vel_hbm, sem.at[1])
    vel.start()
    den.start()
    vel.wait()
    den.wait()


def solution(mesh):
    gy, gz = mesh.shape["gy"], mesh.shape["gz"]

    def local(populations, solid_mask, body_force):
        planes, across, length = solid_mask.shape
        rows = len(Y_SET[1])
        wide = length + 2 * W
        both = pl.pallas_call(
            functools.partial(kernel, gy, gz),
            out_shape=jax.ShapeDtypeStruct((4, planes, across, length), jnp.float32),
            in_specs=[
                pl.BlockSpec(memory_space=pltpu.HBM),
                pl.BlockSpec(memory_space=pltpu.HBM),
                pl.BlockSpec(memory_space=pltpu.SMEM),
            ],
            out_specs=pl.BlockSpec(memory_space=pltpu.VMEM),
            scratch_shapes=[
                pltpu.VMEM((planes, 19, across, length), jnp.float32),
                pltpu.VMEM((planes, across, wide), jnp.int32),
                pltpu.VMEM((planes, across, length), jnp.int32),
                pltpu.VMEM((2, 19, planes, across, wide), jnp.float32),
                pltpu.VMEM((STEPS, planes, 2, rows, length), jnp.float32),
                pltpu.VMEM((STEPS, planes, 2, rows, wide), jnp.float32),
                pltpu.VMEM((STEPS, planes, 2, across, W), jnp.float32),
                pltpu.VMEM((STEPS, planes, 6, across, W), jnp.float32),
                pltpu.VMEM((2, planes, length), jnp.int32),
                pltpu.VMEM((2, planes, wide), jnp.int32),
                pltpu.VMEM((2, across, W), jnp.int32),
                pltpu.VMEM((6, across, W), jnp.int32),
                pltpu.SemaphoreType.DMA((1 + planes,)),
                pltpu.SemaphoreType.DMA((STEPS * planes + 1, len(ROUTES))),
                pltpu.SemaphoreType.DMA((STEPS * planes + 1, len(ROUTES))),
            ],
            compiler_params=pltpu.CompilerParams(collective_id=0, has_side_effects=True, vmem_limit_bytes=VMEM_LIMIT),
        )(populations, solid_mask, body_force)
        return pl.pallas_call(
            hand_out,
            out_shape=(
                jax.ShapeDtypeStruct((planes, across, length), jnp.float32),
                jax.ShapeDtypeStruct((3, planes, across, length), jnp.float32),
            ),
            in_specs=[pl.BlockSpec(memory_space=pltpu.VMEM)],
            out_specs=(pl.BlockSpec(memory_space=pl.ANY), pl.BlockSpec(memory_space=pl.ANY)),
            scratch_shapes=[pltpu.SemaphoreType.DMA((2,))],
            compiler_params=pltpu.CompilerParams(vmem_limit_bytes=VMEM_LIMIT),
        )(both)

    return jax.shard_map(
        local,
        mesh=mesh,
        in_specs=(P(None, None, "gy", "gz"), P(None, "gy", "gz"), P()),
        out_specs=(P(None, "gy", "gz"), P(None, None, "gy", "gz")),
        check_vma=False,
    )
```

profile of v0, /device:TPU:1, one launch (start us, length us, event | category | flops | bytes accessed | tf_op | source)
XLA Modules:
  0.0 28.8 jit_solution(12844452559688870988)
XLA Ops:
  0.6 0.0 copy-start
  0.6 1.7 %copy-done = f32[19,4,8,1024]{3,2,1,0:T(8,128)S(1)} copy-done((f32[19,4,8,1024]{3,2,1,0:T(8,128)S(1)}, f32[19,4,8,1024]{3,2,1,0:T(8,128)}, u32[]{:S(2)}) %copy-start) | copy-done | bytes 2490392
  2.3 0.0 copy-start.1
  2.3 0.9 %copy-done.1 = s32[4,8,1024]{2,1,0:T(8,128)S(1)} copy-done((s32[4,8,1024]{2,1,0:T(8,128)S(1)}, s32[4,8,1024]{2,1,0:T(8,128)}, u32[]{:S(2)}) %copy-start.1) | copy-done | bytes 131096
  3.2 0.0 copy-start.2
  3.2 0.7 %copy-done.2 = f32[3]{0:T(128)S(1)} copy-done((f32[3]{0:T(128)S(1)}, f32[3]{0:T(128)}, u32[]{:S(2)}) %copy-start.2) | copy-done | bytes 36
  3.9 24.1 %shard_map.50.both_ref = f32[4,4,8,1024]{3,2,1,0:T(8,128)S(1)} custom-call(f32[19,4,8,1024]{3,2,1,0:T(8,128)S(1)} %copy-done, s32[4,8,1024]{2,1,0:T(8,128)S(1)} %copy-done.1, f32[3]{0:T(128)S(1)} %copy-done.2), custom_call_target="tpu_custom_call" | custom-call | tf_op jit(solution)/shard_map/pallas_call | solution.py:364
  28.0 0.8 %shard_map.51 = (f32[4,8,1024]{2,1,0:T(8,128)}, f32[3,4,8,1024]{3,2,1,0:T(8,128)}) custom-call(f32[4,4,8,1024]{3,2,1,0:T(8,128)S(1)} %shard_map.50.both_ref), custom_call_target="tpu_custom_call" | custom-call | tf_op jit(solution)/shard_map/pallas_call | solution.py:392
Async XLA Ops:
  0.6 1.7 %copy-start = (f32[19,4,8,1024]{3,2,1,0:T(8,128)S(1)}, f32[19,4,8,1024]{3,2,1,0:T(8,128)}, u32[]{:S(2)}) copy-start(f32[19,4,8,1024]{3,2,1,0:T(8,128)} %pop_hbm.1) | copy-start | bytes 7471108
  2.3 0.9 %copy-start.1 = (s32[4,8,1024]{2,1,0:T(8,128)S(1)}, s32[4,8,1024]{2,1,0:T(8,128)}, u32[]{:S(2)}) copy-start(s32[4,8,1024]{2,1,0:T(8,128)} %mask_hbm.1) | copy-start | bytes 393220
  3.2 0.7 %copy-start.2 = (f32[3]{0:T(128)S(1)}, f32[3]{0:T(128)}, u32[]{:S(2)}) copy-start(f32[3]{0:T(128)} %force_ref.1) | copy-start | bytes 40
where the time goes:
time: 29.3 us; the launch traced here: 28.8 us
  Pallas kernels  24.9 us (85%)
  local copies, waits for them, and re-layouts  3.25 us (11%)
  between operations  0.65 us (2%)
    pallas_call x1, Pallas kernels, local(): pl.pallas_call(functools.partial(kernel, gy, gz), out_shape=jax.ShapeDtyp...  24.1 us
    unnamed x6, local copies, waits for them, and re-layouts  3.25 us
    pallas_call x1, Pallas kernels, local(): pl.pallas_call(hand_out, out_shape=(jax.ShapeDtypeStruct((planes, across,...  0.8 us

commit v1 on v0

v1 whole, which is shorter than its diff:
```python
import functools

import jax
import jax.numpy as jnp
from jax import lax
from jax.experimental import pallas as pl
from jax.experimental.pallas import tpu as pltpu
from jax.sharding import PartitionSpec as P

STEPS = 3
W = 128
SEG = 8
VMEM_LIMIT = 60 << 20
LO, HI, ROWS = 8, 16, 24

velocities = [
    (0, 0, 0),
    (1, 0, 0),
    (-1, 0, 0),
    (0, 1, 0),
    (0, -1, 0),
    (0, 0, 1),
    (0, 0, -1),
    (1, 1, 0),
    (-1, -1, 0),
    (1, -1, 0),
    (-1, 1, 0),
    (1, 0, 1),
    (-1, 0, -1),
    (1, 0, -1),
    (-1, 0, 1),
    (0, 1, 1),
    (0, -1, -1),
    (0, 1, -1),
    (0, -1, 1),
]
opposite = [0, 2, 1, 4, 3, 6, 5, 8, 7, 10, 9, 12, 11, 14, 13, 16, 15, 18, 17]
reference_mach = 0.05
ORDER = [5, 11, 14, 15, 3, 7, 10, 17, 6, 12, 13, 16, 4, 8, 9, 18, 0, 1, 2]
SLOT = [ORDER.index(k) for k in range(19)]
Y_RUN = {1: [(3, 5)], -1: [(11, 5)]}
Z_RUN = {1: [(0, 4), (15, 1)], -1: [(7, 5)]}
SIDES = [(1, 0), (-1, 0), (0, 1), (0, -1), (1, 1), (-1, 1), (1, -1), (-1, -1)]
MESH = pl.DeviceIdType.MESH


def moments(f):
    s = [f[2 * a + 1] + f[2 * a + 2] for a in range(9)]
    d = [f[2 * a + 1] - f[2 * a + 2] for a in range(9)]
    axes = s[0] + s[1] + s[2]
    a = (s[3] + s[4], s[5] + s[6], s[7] + s[8])
    edges = a[0] + a[1] + a[2]
    rho = f[0] + axes + edges
    px, py, pz = (d[3] + d[4]) + (d[5] + d[6]), (d[3] - d[4]) + (d[7] + d[8]), (d[5] - d[6]) + (d[7] - d[8])
    jx, jy, jz = d[0] + px, d[1] + py, d[2] + pz
    return s, d, a, (axes, edges), (px, py, pz), rho, jx, jy, jz


def collide(f, force):
    s, d, (axy, axz, ayz), (axes, edges), p, rho, jx, jy, jz = moments(f)
    w = 0.3125 / rho
    vx, vy, vz = jx * w, jy * w, jz * w
    rx, ry, rz = jx * vx, jy * vy, jz * vz
    r = rx + ry + rz
    r3 = r * (0.325 / 0.9375)
    common = rho * (0.625 / 3.0 - 1.3 / 9.0) - r3
    fourth = rho * (0.325 / 9.0) + r3
    out = [None] * 19
    out[0] = (rho * (1.3 / 3.0 - 0.25) - r * 1.92) + (axes * 0.25 + edges * 0.2)
    g = [j * (0.4 / 3.0) + force[i][0] for i, j in enumerate((jx, jy, jz))]
    along = (axy + axz, axy + ayz, axz + ayz)
    for i, ri in enumerate((rx, ry, rz)):
        even = (common + ri * 0.96) + (along[i] * 0.025 - s[i] * 0.125)
        odd = (p[i] * 0.3 - g[i] * 0.25) + force[i][1]
        out[2 * i + 1] = even + odd
        out[2 * i + 2] = even - odd
    planes = (
        (3, axy, rz, vx * jy, g[0], g[1]),
        (5, axz, ry, vx * jz, g[0], g[2]),
        (7, ayz, rx, vy * jz, g[1], g[2]),
    )
    for n, total, across, shear, ga, gb in planes:
        a = (fourth - across * 0.52) - total * 0.075
        b = shear - (s[n] - s[n + 1]) * 0.0625
        e0, e1 = a + b, a - b
        o0, o1 = (ga + gb) - d[n] * 0.3, (ga - gb) - d[n + 1] * 0.3
        out[2 * n + 1], out[2 * n + 2] = e0 + o0, e0 - o0
        out[2 * n + 3], out[2 * n + 4] = e1 + o1, e1 - o1
    return out


def kernel(gy, gz, pop_hbm, mask_hbm, force_hbm, out_ref, raw, raw_mask, force_ref, cells0, cells1, cells2, mask,
           moved_mask, load_sem, send_sem, recv_sem):
    state = (cells0, cells1, cells2)
    planes, across = mask.shape[1], mask.shape[0] - 2
    my, mz = lax.axis_index("gy"), lax.axis_index("gz")

    def peer(dy, dz):
        return {"gy": lax.rem(my + dy + gy, gy), "gz": lax.rem(mz + dz + gz, gz)}

    load_mask = pltpu.make_async_copy(mask_hbm, raw_mask, load_sem.at[0])
    load_force = pltpu.make_async_copy(force_hbm, force_ref, load_sem.at[1])
    load_pop = [pltpu.make_async_copy(pop_hbm.at[:, p], raw.at[:, p], load_sem.at[2 + p]) for p in range(planes)]
    load_mask.start()
    load_force.start()
    for copy in load_pop:
        copy.start()
    barrier = pltpu.get_barrier_semaphore()
    for dy, dz in SIDES:
        pl.semaphore_signal(barrier, inc=1, device_id=peer(dy, dz), device_id_type=MESH)

    lane = lax.broadcasted_iota(jnp.int32, (SEG, W), 1)
    line = slice(LO, HI)

    def remote(source, target, number, side):
        return pltpu.make_async_remote_copy(
            src_ref=source,
            dst_ref=target,
            send_sem=send_sem.at[number],
            recv_sem=recv_sem.at[number],
            device_id=peer(*side),
            device_id_type=MESH,
        )

    def edge(dy):
        return (across, 0) if dy == 1 else (1, across + 1)

    def ends(dz):
        return (slice(HI - 1, HI), slice(LO - 1, LO)) if dz == 1 else (slice(LO, LO + 1), slice(HI, HI + 1))

    count = [0]

    def next_sem():
        count[0] += 1
        return count[0] - 1

    def start(group):
        for copy in group:
            copy.start()
        return group

    def arrive(group):
        for copy in group:
            copy.wait_recv()

    sent = []

    def send_y(buf, dy):
        here, there = edge(dy)
        group = [
            remote(state[buf].at[pl.ds(a, n), here, :, line], state[buf].at[pl.ds(a, n), there, :, line], next_sem(), (dy, 0))
            for a, n in Y_RUN[dy]
        ]
        for dz in (1, -1):
            src, dst = ends(dz)
            k = SLOT[velocities.index((0, dy, dz))]
            group.append(remote(state[buf].at[k, here, :, src], state[buf].at[k, there, :, dst], next_sem(), (dy, dz)))
        sent.append(start(group))
        return group

    def send_z(buf, rows):
        group = []
        for dz in (1, -1):
            src, dst = ends(dz)
            for a, n in Z_RUN[dz]:
                for y0, ny in rows:
                    group.append(
                        remote(
                            state[buf].at[pl.ds(a, n), pl.ds(y0, ny), :, src],
                            state[buf].at[pl.ds(a, n), pl.ds(y0, ny), :, dst],
                            next_sem(),
                            (0, dz),
                        )
                    )
        sent.append(start(group))
        return group

    def send_mask():
        group = []
        for dy in (1, -1):
            here, there = edge(dy)
            group.append(remote(mask.at[here, :, line], mask.at[there, :, line], next_sem(), (dy, 0)))
        for dz in (1, -1):
            src, dst = ends(dz)
            group.append(remote(mask.at[pl.ds(1, across), :, src], mask.at[pl.ds(1, across), :, dst], next_sem(), (0, dz)))
            for dy in (1, -1):
                here, there = edge(dy)
                group.append(remote(mask.at[here, :, src], mask.at[there, :, dst], next_sem(), (dy, dz)))
        sent.append(start(group))
        return group

    def along_z(load, cz):
        v = load(0)
        if cz == 1:
            return pltpu.roll(jnp.where(lane == W - 1, load(-1), v), 1, 1)
        if cz == -1:
            return pltpu.roll(jnp.where(lane == 0, load(1), v), W - 1, 1)
        return v

    def move_mask(y):
        for p in range(planes):
            for i, cz in enumerate((1, -1)):
                moved_mask[i, y, p] = along_z(lambda o: mask[y, p, LO + o : HI + o, :], cz)

    def streamed(buf, p, y):
        f = []
        for k in range(19):
            cx, cy, cz = velocities[k]
            here = state[buf][SLOT[opposite[k]], y, p, line, :]
            q = p - cx
            if k == 0 or not 0 <= q < planes:
                f.append(here)
                continue
            moved = along_z(lambda o: state[buf][SLOT[k], y - cy, q, LO + o : HI + o, :], cz)
            blocked = mask[y - cy, q, line, :] if cz == 0 else moved_mask[(1 - cz) // 2, y - cy, q]
            f.append(jnp.where(blocked != 0, here, moved))
        return f

    def relax(buf, f, p, y):
        for k, value in enumerate(collide(f, force)):
            state[buf][SLOT[k], y, p, line, :] = value

    load_mask.wait()
    for p in range(planes):
        for y in range(across):
            mask[y + 1, p, line, :] = raw_mask[p, pl.ds(y, SEG, stride=across), :]
    load_force.wait()
    force = [(force_ref[i] * (1.0 / 12.0), force_ref[i] * 0.1875) for i in range(3)]

    group = max(u for u in (4, 2, 1) if across % u == 0)
    for p in range(planes):
        load_pop[p].wait()

        def first(i, carry, p=p):
            for n in range(group):
                y = i * group + n
                relax(0, [raw[k, p, pl.ds(y, SEG, stride=across), :] for k in range(19)], p, y + 1)
            return carry

        lax.fori_loop(0, across // group, first, 0)

    pl.semaphore_wait(barrier, len(SIDES))
    coming_mask = send_mask()
    coming_y = {dy: send_y(0, dy) for dy in (1, -1)}
    coming_z = send_z(0, [(1, across)])

    arrive(coming_mask)

    def shift(y, carry):
        move_mask(y)
        return carry

    lax.fori_loop(0, across + 2, shift, 0)

    def final(buf, y):
        for p in range(planes):
            rho, jx, jy, jz = moments(streamed(buf, p, y))[-4:]
            fluid = (1 - mask[y, p, line, :]).astype(jnp.float32)
            scale = fluid * (1.0 / reference_mach) / rho
            spot = pl.ds(y - 1, SEG, stride=across)
            out_ref[0, p, spot, :] = rho * fluid
            out_ref[1, p, spot, :] = jx * scale
            out_ref[2, p, spot, :] = jy * scale
            out_ref[3, p, spot, :] = jz * scale

    def middle(step, y):
        for p in range(planes):
            relax(step + 1, streamed(step, p, y), p, y)

    def interior(block):
        def body(y, carry):
            block(y)
            return carry

        lax.fori_loop(3, across - 1, body, 0)

    near, far = coming_z, coming_z
    for step in range(STEPS - 1):
        arrive(near)
        later_y = {}
        for dy, y in ((-1, 1), (1, across)):
            arrive(coming_y[-dy])
            middle(step, y)
            later_y[dy] = send_y(step + 1, dy)
        if far is not near:
            arrive(far)
        middle(step, 2)
        middle(step, across - 1)
        near = send_z(step + 1, [(1, 2), (across - 1, 2)])
        interior(functools.partial(middle, step))
        far = send_z(step + 1, [(3, across - 4)])
        coming_y = later_y

    last = STEPS - 1
    arrive(near)
    arrive(far)
    final(last, 2)
    final(last, across - 1)
    interior(functools.partial(final, last))
    for dy, y in ((-1, 1), (1, across)):
        arrive(coming_y[-dy])
        final(last, y)
    for group in sent:
        for copy in group:
            copy.wait_send()


def hand_out(both_ref, den_hbm, vel_hbm, sem):
    den = pltpu.make_async_copy(both_ref.at[0], den_hbm, sem.at[0])
    vel = pltpu.make_async_copy(both_ref.at[pl.ds(1, 3)], vel_hbm, sem.at[1])
    vel.start()
    den.start()
    vel.wait()
    den.wait()


def solution(mesh):
    gy, gz = mesh.shape["gy"], mesh.shape["gz"]

    def tiles(x, across):
        lead = x.shape[:-2]
        x = x.reshape(*lead, across, SEG, W)
        return jnp.swapaxes(x, -3, -2).reshape(*lead, SEG * across, W)

    def lines(x, across):
        lead = x.shape[:-2]
        x = x.reshape(*lead, SEG, across, W)
        return jnp.swapaxes(x, -3, -2).reshape(*lead, across, SEG * W)

    def local(populations, solid_mask, body_force):
        planes, across, length = solid_mask.shape
        if length != SEG * W or across < 6:
            raise ValueError("unsupported block")
        messages = 64
        both = pl.pallas_call(
            functools.partial(kernel, gy, gz),
            out_shape=jax.ShapeDtypeStruct((4, planes, SEG * across, W), jnp.float32),
            in_specs=[pl.BlockSpec(memory_space=pltpu.HBM)] * 3,
            out_specs=pl.BlockSpec(memory_space=pltpu.VMEM),
            scratch_shapes=[
                pltpu.VMEM((19, planes, SEG * across, W), jnp.float32),
                pltpu.VMEM((planes, SEG * across, W), jnp.int32),
                pltpu.SMEM((3,), jnp.float32),
                *[pltpu.VMEM((19, across + 2, planes, ROWS, W), jnp.float32)] * STEPS,
                pltpu.VMEM((across + 2, planes, ROWS, W), jnp.int32),
                pltpu.VMEM((2, across + 2, planes, SEG, W), jnp.int32),
                pltpu.SemaphoreType.DMA((2 + planes,)),
                pltpu.SemaphoreType.DMA((messages,)),
                pltpu.SemaphoreType.DMA((messages,)),
            ],
            compiler_params=pltpu.CompilerParams(collective_id=0, has_side_effects=True, vmem_limit_bytes=VMEM_LIMIT),
        )(tiles(populations, across), tiles(solid_mask, across), body_force)
        density, velocity = pl.pallas_call(
            hand_out,
            out_shape=(
                jax.ShapeDtypeStruct((planes, SEG * across, W), jnp.float32),
                jax.ShapeDtypeStruct((3, planes, SEG * across, W), jnp.float32),
            ),
            in_specs=[pl.BlockSpec(memory_space=pltpu.VMEM)],
            out_specs=(pl.BlockSpec(memory_space=pl.ANY), pl.BlockSpec(memory_space=pl.ANY)),
            scratch_shapes=[pltpu.SemaphoreType.DMA((2,))],
            compiler_params=pltpu.CompilerParams(vmem_limit_bytes=VMEM_LIMIT),
        )(both)
        return lines(density, across), lines(velocity, across)

    return jax.shard_map(
        local,
        mesh=mesh,
        in_specs=(P(None, None, "gy", "gz"), P(None, "gy", "gz"), P()),
        out_specs=(P(None, "gy", "gz"), P(None, None, "gy", "gz")),
        check_vma=False,
    )
```

time: 29.3 us -> 27.7 us (0.945)
  the two profiles are of different devices: /device:TPU:1 before, /device:TPU:0 now
where the time goes in v1:
time: 27.7 us; the launch traced here: 27.5 us
  Pallas kernels  26.9 us (97%)
  between operations  0.64 us (2%)
    pallas_call x1, Pallas kernels, local(): pl.pallas_call(functools.partial(kernel, gy, gz), out_shape=jax.ShapeDtyp...  25 us
    pallas_call x1, Pallas kernels, local(): pl.pallas_call(hand_out, out_shape=(jax.ShapeDtypeStruct((planes, SEG * a...  1.84 us

profile of v1, /device:TPU:0, one launch (start us, length us, event | category | flops | bytes accessed | tf_op | source)
XLA Modules:
  0.0 27.5 jit_solution(16328335514216486608)
XLA Ops:
  0.6 25.0 %shard_map.50.both_ref = f32[4,4,64,128]{3,2,1,0:T(8,128)} custom-call(f32[19,4,64,128]{3,2,1,0:T(8,128)} %bitcast.20, s32[4,64,128]{2,1,0:T(8,128)} %bitcast.21, f32[3]{0:T(128)} %force_hbm.1), custom_call_target="tpu_custom_call" | custom-call | tf_op jit(solution)/shard_map/pallas_call | solution.py:335
  25.7 1.8 %shard_map.51 = (f32[4,64,128]{2,1,0:T(8,128)}, f32[3,4,64,128]{3,2,1,0:T(8,128)}) custom-call(f32[4,4,64,128]{3,2,1,0:T(8,128)} %shard_map.50.both_ref), custom_call_target="tpu_custom_call" | custom-call | tf_op jit(solution)/shard_map/pallas_call | solution.py:353

commit v2 on v1

--- a/solution.py
+++ b/solution.py
@@ -39,7 +39,7 @@
 ORDER = [5, 11, 14, 15, 3, 7, 10, 17, 6, 12, 13, 16, 4, 8, 9, 18, 0, 1, 2]
 SLOT = [ORDER.index(k) for k in range(19)]
 Y_RUN = {1: [(3, 5)], -1: [(11, 5)]}
-Z_RUN = {1: [(0, 4), (15, 1)], -1: [(7, 5)]}
+Z_SET = {dz: [k for k in range(19) if velocities[k][2] == dz] for dz in (1, -1)}
 SIDES = [(1, 0), (-1, 0), (0, 1), (0, -1), (1, 1), (-1, 1), (1, -1), (-1, -1)]
 MESH = pl.DeviceIdType.MESH
 
@@ -90,9 +90,9 @@
 
 
 def kernel(gy, gz, pop_hbm, mask_hbm, force_hbm, out_ref, raw, raw_mask, force_ref, cells0, cells1, cells2, mask,
-           moved_mask, load_sem, send_sem, recv_sem):
+           moved_mask, zs, zh, mzs, mzh, load_sem, send_sem, recv_sem):
     state = (cells0, cells1, cells2)
-    planes, across = mask.shape[1], mask.shape[0] - 2
+    planes, across = pop_hbm.shape[1], pop_hbm.shape[2] // SEG
     my, mz = lax.axis_index("gy"), lax.axis_index("gz")
 
     def peer(dy, dz):
@@ -145,49 +145,93 @@
 
     sent = []
 
+    def entries(ref, lead):
+        return ref.reshape(*lead, across + 2, planes, ROWS, W)
+
+    views = [entries(ref, (19,)) for ref in state]
+    mask_view = entries(mask, ())
+
+    def at(y, p, row=LO):
+        base = (y * planes + p) * ROWS
+        return (base if isinstance(y, int) else pl.multiple_of(base, 8)) + row
+
     def send_y(buf, dy):
         here, there = edge(dy)
-        group = [
-            remote(state[buf].at[pl.ds(a, n), here, :, line], state[buf].at[pl.ds(a, n), there, :, line], next_sem(), (dy, 0))
-            for a, n in Y_RUN[dy]
-        ]
+        group = []
         for dz in (1, -1):
             src, dst = ends(dz)
             k = SLOT[velocities.index((0, dy, dz))]
-            group.append(remote(state[buf].at[k, here, :, src], state[buf].at[k, there, :, dst], next_sem(), (dy, dz)))
+            group.append(remote(views[buf].at[k, here, :, src], views[buf].at[k, there, :, dst], next_sem(), (dy, dz)))
+        for a, n in Y_RUN[dy]:
+            source, target = views[buf].at[pl.ds(a, n), here, :, line], views[buf].at[pl.ds(a, n), there, :, line]
+            group.append(remote(source, target, next_sem(), (dy, 0)))
         sent.append(start(group))
         return group
 
-    def send_z(buf, rows):
-        group = []
-        for dz in (1, -1):
-            src, dst = ends(dz)
-            for a, n in Z_RUN[dz]:
-                for y0, ny in rows:
-                    group.append(
-                        remote(
-                            state[buf].at[pl.ds(a, n), pl.ds(y0, ny), :, src],
-                            state[buf].at[pl.ds(a, n), pl.ds(y0, ny), :, dst],
-                            next_sem(),
-                            (0, dz),
-                        )
-                    )
-        sent.append(start(group))
-        return group
+    def send_z(out, into, lines_of, starts, group):
+        copies = []
+        for i, dz in enumerate((1, -1)):
+            refs = lines_of(dz)
+            packed = jnp.zeros((SEG, W), out.dtype)
+            row = HI - 1 if dz == 1 else LO
+            for j, (load, y) in enumerate((load, y) for load, _ in refs for y in starts):
+                shift = (j + 1 if dz == 1 else j) % W
+                v = load(pl.ds(at(y, 0, row), SEG, stride=ROWS))
+                packed = jnp.where(lane == j, pltpu.roll(v, shift, 1) if shift else v, packed)
+            out[group, i] = packed
+            copies.append(remote(out.at[group, i], into.at[group, i], next_sem(), (0, dz)))
+        sent.append(start(copies))
+
+        def done():
+            for i, dz in enumerate((1, -1)):
+                copies[i].wait_recv()
+                row = LO - 1 if dz == 1 else HI
+                packed = into[group, i]
+                for j, (store, y) in enumerate((store, y) for _, store in lines_of(dz) for y in starts):
+                    shift = (W - 1 - j if dz == 1 else W - j) % W
+                    store(pl.ds(at(y, 0, row), SEG, stride=ROWS), pltpu.roll(packed, shift, 1) if shift else packed)
+
+        return done
+
+    def lines_of(ref):
+        def pick(dz):
+            result = []
+            for k in Z_SET[dz]:
+                slot = SLOT[k]
+
+                def load(rows, slot=slot):
+                    return ref[slot, rows, :]
+
+                def store(rows, value, slot=slot):
+                    ref[slot, rows, :] = value
+
+                result.append((load, store))
+            return result
+
+        return pick
+
+    def mask_lines(dz):
+        def store(rows, value):
+            mask[rows, :] = value
+
+        return [(lambda rows: mask[rows, :], store)]
+
+    near_rows, far_rows = [1, across - 1], list(range(3, across - 1, 2))
+
+    def send_state(buf, rows):
+        group = buf * 2 + (0 if rows is near_rows else 1)
+        return send_z(zs, zh, lines_of(state[buf]), rows, group)
 
     def send_mask():
         group = []
         for dy in (1, -1):
             here, there = edge(dy)
-            group.append(remote(mask.at[here, :, line], mask.at[there, :, line], next_sem(), (dy, 0)))
-        for dz in (1, -1):
-            src, dst = ends(dz)
-            group.append(remote(mask.at[pl.ds(1, across), :, src], mask.at[pl.ds(1, across), :, dst], next_sem(), (0, dz)))
-            for dy in (1, -1):
-                here, there = edge(dy)
-                group.append(remote(mask.at[here, :, src], mask.at[there, :, dst], next_sem(), (dy, dz)))
+            for dz in (1, -1):
+                src, dst = ends(dz)
+                group.append(remote(mask_view.at[here, :, src], mask_view.at[there, :, dst], next_sem(), (dy, dz)))
+            group.append(remote(mask_view.at[here, :, line], mask_view.at[there, :, line], next_sem(), (dy, 0)))
         sent.append(start(group))
-        return group
+        return group, send_z(mzs, mzh, mask_lines, near_rows + far_rows, 0)
 
     def along_z(load, cz):
         v = load(0)
@@ -200,30 +244,30 @@
     def move_mask(y):
         for p in range(planes):
             for i, cz in enumerate((1, -1)):
-                moved_mask[i, y, p] = along_z(lambda o: mask[y, p, LO + o : HI + o, :], cz)
+                moved_mask[i, y, p] = along_z(lambda o: mask[pl.ds(at(y, p, LO + o), SEG), :], cz)
 
     def streamed(buf, p, y):
         f = []
         for k in range(19):
             cx, cy, cz = velocities[k]
-            here = state[buf][SLOT[opposite[k]], y, p, line, :]
+            here = state[buf][SLOT[opposite[k]], pl.ds(at(y, p), SEG), :]
             q = p - cx
             if k == 0 or not 0 <= q < planes:
                 f.append(here)
                 continue
-            moved = along_z(lambda o: state[buf][SLOT[k], y - cy, q, LO + o : HI + o, :], cz)
-            blocked = mask[y - cy, q, line, :] if cz == 0 else moved_mask[(1 - cz) // 2, y - cy, q]
+            moved = along_z(lambda o: state[buf][SLOT[k], pl.ds(at(y - cy, q, LO + o), SEG), :], cz)
+            blocked = mask[pl.ds(at(y - cy, q), SEG), :] if cz == 0 else moved_mask[(1 - cz) // 2, y - cy, q]
             f.append(jnp.where(blocked != 0, here, moved))
         return f
 
     def relax(buf, f, p, y):
         for k, value in enumerate(collide(f, force)):
-            state[buf][SLOT[k], y, p, line, :] = value
+            state[buf][SLOT[k], pl.ds(at(y, p), SEG), :] = value
 
     load_mask.wait()
     for p in range(planes):
         for y in range(across):
-            mask[y + 1, p, line, :] = raw_mask[p, pl.ds(y, SEG, stride=across), :]
+            mask[pl.ds(at(y + 1, p), SEG), :] = raw_mask[p, pl.ds(y, SEG, stride=across), :]
     load_force.wait()
     force = [(force_ref[i] * (1.0 / 12.0), force_ref[i] * 0.1875) for i in range(3)]
 
@@ -240,10 +284,11 @@
         lax.fori_loop(0, across // group, first, 0)
 
     pl.semaphore_wait(barrier, len(SIDES))
-    coming_mask = send_mask()
+    coming_mask, mask_done = send_mask()
     coming_y = {dy: send_y(0, dy) for dy in (1, -1)}
-    coming_z = send_z(0, [(1, across)])
-
+    near, far = send_state(0, near_rows), send_state(0, far_rows)
+
+    mask_done()
     arrive(coming_mask)
 
     def shift(y, carry):
@@ -255,7 +300,7 @@
     def final(buf, y):
         for p in range(planes):
             rho, jx, jy, jz = moments(streamed(buf, p, y))[-4:]
-            fluid = (1 - mask[y, p, line, :]).astype(jnp.float32)
+            fluid = (1 - mask[pl.ds(at(y, p), SEG), :]).astype(jnp.float32)
             scale = fluid * (1.0 / reference_mach) / rho
             spot = pl.ds(y - 1, SEG, stride=across)
             out_ref[0, p, spot, :] = rho * fluid
@@ -274,26 +319,24 @@
 
         lax.fori_loop(3, across - 1, body, 0)
 
-    near, far = coming_z, coming_z
     for step in range(STEPS - 1):
-        arrive(near)
+        near()
         later_y = {}
         for dy, y in ((-1, 1), (1, across)):
             arrive(coming_y[-dy])
             middle(step, y)
             later_y[dy] = send_y(step + 1, dy)
-        if far is not near:
-            arrive(far)
+        far()
         middle(step, 2)
         middle(step, across - 1)
-        near = send_z(step + 1, [(1, 2), (across - 1, 2)])
+        near = send_state(step + 1, near_rows)
         interior(functools.partial(middle, step))
-        far = send_z(step + 1, [(3, across - 4)])
+        far = send_state(step + 1, far_rows)
         coming_y = later_y
 
     last = STEPS - 1
-    arrive(near)
-    arrive(far)
+    near()
+    far()
     final(last, 2)
     final(last, across - 1)
     interior(functools.partial(final, last))
@@ -329,7 +372,7 @@
 
     def local(populations, solid_mask, body_force):
         planes, across, length = solid_mask.shape
-        if length != SEG * W or across < 6:
+        if length != SEG * W or across < 6 or across % 2 or 2 * planes != SEG:
             raise ValueError("unsupported block")
         messages = 64
         both = pl.pallas_call(
@@ -341,9 +384,13 @@
                 pltpu.VMEM((19, planes, SEG * across, W), jnp.float32),
                 pltpu.VMEM((planes, SEG * across, W), jnp.int32),
                 pltpu.SMEM((3,), jnp.float32),
-                *[pltpu.VMEM((19, across + 2, planes, ROWS, W), jnp.float32)] * STEPS,
-                pltpu.VMEM((across + 2, planes, ROWS, W), jnp.int32),
+                *[pltpu.VMEM((19, (across + 2) * planes * ROWS, W), jnp.float32)] * STEPS,
+                pltpu.VMEM(((across + 2) * planes * ROWS, W), jnp.int32),
                 pltpu.VMEM((2, across + 2, planes, SEG, W), jnp.int32),
+                pltpu.VMEM((2 * STEPS, 2, SEG, W), jnp.float32),
+                pltpu.VMEM((2 * STEPS, 2, SEG, W), jnp.float32),
+                pltpu.VMEM((1, 2, SEG, W), jnp.int32),
+                pltpu.VMEM((1, 2, SEG, W), jnp.int32),
                 pltpu.SemaphoreType.DMA((2 + planes,)),
                 pltpu.SemaphoreType.DMA((messages,)),
                 pltpu.SemaphoreType.DMA((messages,)),
@@ -359,7 +406,7 @@
             in_specs=[pl.BlockSpec(memory_space=pltpu.VMEM)],
             out_specs=(pl.BlockSpec(memory_space=pl.ANY), pl.BlockSpec(memory_space=pl.ANY)),
             scratch_shapes=[pltpu.SemaphoreType.DMA((2,))],
-            compiler_params=pltpu.CompilerParams(vmem_limit_bytes=VMEM_LIMIT),
+            compiler_params=pltpu.CompilerParams(vmem_limit_bytes=1 << 20),
         )(both)
         return lines(density, across), lines(velocity, across)
 

time: 27.7 us -> 26.2 us (0.946)
  Pallas kernels: 26.9 us -> 24.3 us
  local copies, waits for them, and re-layouts: 0 us -> 1.03 us
    pallas_call x1, Pallas kernels: 25 us -> 23.5 us  [local(): pl.pallas_call(functools.partial(kernel, gy, gz), out_shape=jax.ShapeDtyp...]
    pallas_call x1, Pallas kernels: 1.84 us -> 0.8 us  [local(): pl.pallas_call(hand_out, out_shape=(jax.ShapeDtypeStruct((planes, SEG * a...]
    unnamed x0 -> x2, local copies, waits for them, and re-layouts: none -> 1.03 us
where the time goes in v2:
time: 26.2 us; the launch traced here: 26 us
  Pallas kernels  24.3 us (93%)
  local copies, waits for them, and re-layouts  1.03 us (4%)
  between operations  0.65 us (2%)
    pallas_call x1, Pallas kernels, local(): pl.pallas_call(functools.partial(kernel, gy, gz), out_shape=jax.ShapeDtyp...  23.5 us
    unnamed x2, local copies, waits for them, and re-layouts  1.03 us
    pallas_call x1, Pallas kernels, local(): pl.pallas_call(hand_out, out_shape=(jax.ShapeDtypeStruct((planes, SEG * a...  0.8 us

profile of v2, /device:TPU:0, one launch (start us, length us, event | category | flops | bytes accessed | tf_op | source)
XLA Modules:
  0.0 26.0 jit_solution(12523111205716074822)
XLA Ops:
  0.6 23.5 %shard_map.50.both_ref = f32[4,4,64,128]{3,2,1,0:T(8,128)} custom-call(f32[19,4,64,128]{3,2,1,0:T(8,128)} %bitcast.20, s32[4,64,128]{2,1,0:T(8,128)} %bitcast.21, f32[3]{0:T(128)} %force_hbm.1), custom_call_target="tpu_custom_call" | custom-call | tf_op jit(solution)/shard_map/pallas_call | solution.py:378
  24.1 0.0 copy-start
  24.1 1.0 %copy-done = f32[4,4,64,128]{3,2,1,0:T(8,128)S(1)} copy-done((f32[4,4,64,128]{3,2,1,0:T(8,128)S(1)}, f32[4,4,64,128]{3,2,1,0:T(8,128)}, u32[]{:S(2)}) %copy-start) | copy-done | bytes 524312
  25.2 0.8 %shard_map.51 = (f32[4,64,128]{2,1,0:T(8,128)}, f32[3,4,64,128]{3,2,1,0:T(8,128)}) custom-call(f32[4,4,64,128]{3,2,1,0:T(8,128)S(1)} %copy-done), custom_call_target="tpu_custom_call" | custom-call | tf_op jit(solution)/shard_map/pallas_call | solution.py:400
Async XLA Ops:
  24.1 1.0 %copy-start = (f32[4,4,64,128]{3,2,1,0:T(8,128)S(1)}, f32[4,4,64,128]{3,2,1,0:T(8,128)}, u32[]{:S(2)}) copy-start(f32[4,4,64,128]{3,2,1,0:T(8,128)} %shard_map.50.both_ref) | copy-start | bytes 1572868

commit v3 on v2

--- a/solution.py
+++ b/solution.py
@@ -271,22 +271,29 @@
     load_force.wait()
     force = [(force_ref[i] * (1.0 / 12.0), force_ref[i] * 0.1875) for i in range(3)]
 
-    group = max(u for u in (4, 2, 1) if across % u == 0)
+    def first(p, y):
+        relax(0, [raw[k, p, pl.ds(y - 1, SEG, stride=across), :] for k in range(19)], p, y)
+
     for p in range(planes):
         load_pop[p].wait()
-
-        def first(i, carry, p=p):
-            for n in range(group):
-                y = i * group + n
-                relax(0, [raw[k, p, pl.ds(y, SEG, stride=across), :] for k in range(19)], p, y + 1)
-            return carry
-
-        lax.fori_loop(0, across // group, first, 0)
+        first(p, 1)
+        first(p, across)
 
     pl.semaphore_wait(barrier, len(SIDES))
     coming_mask, mask_done = send_mask()
     coming_y = {dy: send_y(0, dy) for dy in (1, -1)}
-    near, far = send_state(0, near_rows), send_state(0, far_rows)
+    for p in range(planes):
+        first(p, 2)
+        first(p, across - 1)
+    near = send_state(0, near_rows)
+
+    def rest(y, carry):
+        for p in range(planes):
+            first(p, y)
+        return carry
+
+    lax.fori_loop(3, across - 1, rest, 0)
+    far = send_state(0, far_rows)
 
     mask_done()
     arrive(coming_mask)
@@ -377,7 +384,7 @@
         messages = 64
         both = pl.pallas_call(
             functools.partial(kernel, gy, gz),
-            out_shape=jax.ShapeDtypeStruct((4, planes, SEG * across, W), jnp.float32),
+            out_shape=pltpu.VMEM((4, planes, SEG * across, W), jnp.float32),
             in_specs=[pl.BlockSpec(memory_space=pltpu.HBM)] * 3,
             out_specs=pl.BlockSpec(memory_space=pltpu.VMEM),
             scratch_shapes=[
@@ -396,7 +403,7 @@
                 pltpu.SemaphoreType.DMA((messages,)),
             ],
             compiler_params=pltpu.CompilerParams(collective_id=0, has_side_effects=True, vmem_limit_bytes=VMEM_LIMIT),
-        )(tiles(populations, across), tiles(solid_mask, across), body_force)
+        )(*[pltpu.with_memory_space_constraint(x, pltpu.HBM) for x in (tiles(populations, across), tiles(solid_mask, across), body_force)])
         density, velocity = pl.pallas_call(
             hand_out,
             out_shape=(

time: 26.2 us -> 24.3 us (0.927)
  local copies, waits for them, and re-layouts: 1.03 us -> 0 us
  Pallas kernels: 24.3 us -> 23.5 us
    unnamed x2 -> x0, local copies, waits for them, and re-layouts: 1.03 us -> none
    pallas_call x1, Pallas kernels: 23.5 us -> 22.7 us  [local(): pl.pallas_call(functools.partial(kernel, gy, gz), out_shape=pltpu.VMEM((4...]
where the time goes in v3:
time: 24.3 us; the launch traced here: 24.2 us
  Pallas kernels  23.5 us (97%)
  between operations  0.64 us (3%)
    pallas_call x1, Pallas kernels, local(): pl.pallas_call(functools.partial(kernel, gy, gz), out_shape=pltpu.VMEM((4...  22.7 us
    pallas_call x1, Pallas kernels, local(): pl.pallas_call(hand_out, out_shape=(jax.ShapeDtypeStruct((planes, SEG * a...  0.8 us

profile of v3, /device:TPU:0, one launch (start us, length us, event | category | flops | bytes accessed | tf_op | source)
XLA Modules:
  0.0 24.2 jit_solution(15721784524213164884)
XLA Ops:
  0.6 22.7 %shard_map.50.both_ref = f32[4,4,64,128]{3,2,1,0:T(8,128)S(1)} custom-call(f32[19,4,64,128]{3,2,1,0:T(8,128)} %bitcast.20, s32[4,64,128]{2,1,0:T(8,128)} %bitcast.21, f32[3]{0:T(128)} %force_hbm.1), custom_call_target="tpu_custom_call" | custom-call | tf_op jit(solution)/shard_map/pallas_call | solution.py:385
  23.4 0.8 %shard_map.51 = (f32[4,64,128]{2,1,0:T(8,128)}, f32[3,4,64,128]{3,2,1,0:T(8,128)}) custom-call(f32[4,4,64,128]{3,2,1,0:T(8,128)S(1)} %shard_map.50.both_ref), custom_call_target="tpu_custom_call" | custom-call | tf_op jit(solution)/shard_map/pallas_call | solution.py:407

commit v4 on v1

v4 whole, which is shorter than its diff:
```python
import functools

import jax
import jax.numpy as jnp
from jax import lax
from jax.experimental import pallas as pl
from jax.experimental.pallas import tpu as pltpu
from jax.sharding import PartitionSpec as P

STEPS = 3
W = 128
SEG = 8
VMEM_LIMIT = 60 << 20
LO, HI, ROWS = 8, 16, 24
DEEP, STRIP, SPARE = 2, 3, 5

velocities = [
    (0, 0, 0),
    (1, 0, 0),
    (-1, 0, 0),
    (0, 1, 0),
    (0, -1, 0),
    (0, 0, 1),
    (0, 0, -1),
    (1, 1, 0),
    (-1, -1, 0),
    (1, -1, 0),
    (-1, 1, 0),
    (1, 0, 1),
    (-1, 0, -1),
    (1, 0, -1),
    (-1, 0, 1),
    (0, 1, 1),
    (0, -1, -1),
    (0, 1, -1),
    (0, -1, 1),
]
opposite = [0, 2, 1, 4, 3, 6, 5, 8, 7, 10, 9, 12, 11, 14, 13, 16, 15, 18, 17]
reference_mach = 0.05
ORDER = [5, 11, 14, 15, 3, 7, 10, 17, 6, 12, 13, 16, 4, 8, 9, 18, 0, 1, 2]
SLOT = [ORDER.index(k) for k in range(19)]
Y_RUN = {1: (3, 5), -1: (11, 5)}
Y_SET = {dy: [k for k in ORDER if velocities[k][1] == dy] for dy in (1, -1)}
PART = {dy: [k for k in ORDER if velocities[k][1] != -dy] for dy in (1, -1)}
SIDES = [(1, 0), (-1, 0), (0, 1), (0, -1)]
MESH = pl.DeviceIdType.MESH


def moments(f):
    s = [f[2 * a + 1] + f[2 * a + 2] for a in range(9)]
    d = [f[2 * a + 1] - f[2 * a + 2] for a in range(9)]
    axes = s[0] + s[1] + s[2]
    a = (s[3] + s[4], s[5] + s[6], s[7] + s[8])
    edges = a[0] + a[1] + a[2]
    rho = f[0] + axes + edges
    px, py, pz = (d[3] + d[4]) + (d[5] + d[6]), (d[3] - d[4]) + (d[7] + d[8]), (d[5] - d[6]) + (d[7] - d[8])
    jx, jy, jz = d[0] + px, d[1] + py, d[2] + pz
    return s, d, a, (axes, edges), (px, py, pz), rho, jx, jy, jz


def collide(f, force):
    s, d, (axy, axz, ayz), (axes, edges), p, rho, jx, jy, jz = moments(f)
    w = 0.3125 / rho
    vx, vy, vz = jx * w, jy * w, jz * w
    rx, ry, rz = jx * vx, jy * vy, jz * vz
    r = rx + ry + rz
    r3 = r * (0.325 / 0.9375)
    common = rho * (0.625 / 3.0 - 1.3 / 9.0) - r3
    fourth = rho * (0.325 / 9.0) + r3
    out = [None] * 19
    out[0] = (rho * (1.3 / 3.0 - 0.25) - r * 1.92) + (axes * 0.25 + edges * 0.2)
    g = [j * (0.4 / 3.0) + force[i][0] for i, j in enumerate((jx, jy, jz))]
    along = (axy + axz, axy + ayz, axz + ayz)
    for i, ri in enumerate((rx, ry, rz)):
        even = (common + ri * 0.96) + (along[i] * 0.025 - s[i] * 0.125)
        odd = (p[i] * 0.3 - g[i] * 0.25) + force[i][1]
        out[2 * i + 1] = even + odd
        out[2 * i + 2] = even - odd
    planes = (
        (3, axy, rz, vx * jy, g[0], g[1]),
        (5, axz, ry, vx * jz, g[0], g[2]),
        (7, ayz, rx, vy * jz, g[1], g[2]),
    )
    for n, total, across, shear, ga, gb in planes:
        a = (fourth - across * 0.52) - total * 0.075
        b = shear - (s[n] - s[n + 1]) * 0.0625
        e0, e1 = a + b, a - b
        o0, o1 = (ga + gb) - d[n] * 0.3, (ga - gb) - d[n + 1] * 0.3
        out[2 * n + 1], out[2 * n + 2] = e0 + o0, e0 - o0
        out[2 * n + 3], out[2 * n + 4] = e1 + o1, e1 - o1
    return out


def kernel(gy, gz, pop_hbm, mask_hbm, force_hbm, out_ref, raw, raw_mask, force_ref, cells0, cells1, cells2, strip0, strip1,
           mask, moved_mask, strip_mask, strip_flag, zs, zh, mzs, mzh, part, part_h, spart, spart_h, third, third_h,
           load_sem, send_sem, recv_sem):
    state, strips = (cells0, cells1, cells2), (strip0, strip1)
    planes, across = pop_hbm.shape[1], pop_hbm.shape[2] // SEG
    total = across + 2 * DEEP
    my, mz = lax.axis_index("gy"), lax.axis_index("gz")

    def peer(dy, dz):
        return {"gy": lax.rem(my + dy + gy, gy), "gz": lax.rem(mz + dz + gz, gz)}

    load_mask = pltpu.make_async_copy(mask_hbm, raw_mask, load_sem.at[0])
    load_force = pltpu.make_async_copy(force_hbm, force_ref, load_sem.at[1])
    load_pop = [pltpu.make_async_copy(pop_hbm.at[:, p], raw.at[:, p], load_sem.at[2 + p]) for p in range(planes)]
    load_mask.start()
    load_force.start()
    for copy in load_pop:
        copy.start()
    barrier = pltpu.get_barrier_semaphore()
    for dy, dz in SIDES:
        pl.semaphore_signal(barrier, inc=1, device_id=peer(dy, dz), device_id_type=MESH)

    lane = lax.broadcasted_iota(jnp.int32, (SEG, W), 1)
    plane_of = lax.rem(lax.broadcasted_iota(jnp.int32, (SEG, W), 0), planes)
    triple = (lane * 43) >> 7
    line = slice(LO, HI)
    count = [0]
    sent = []

    def send(source, target, side):
        copy = pltpu.make_async_remote_copy(
            src_ref=source,
            dst_ref=target,
            send_sem=send_sem.at[count[0]],
            recv_sem=recv_sem.at[count[0]],
            device_id=peer(*side),
            device_id_type=MESH,
        )
        count[0] += 1
        copy.start()
        sent.append(copy)
        return copy

    def arrive(copies):
        for copy in copies:
            copy.wait_recv()

    def view(ref, lead):
        return ref.reshape(*lead, total * planes + 2 * SPARE, ROWS, W)

    views = [view(ref, (19,)) for ref in state]
    mask_view = view(mask, ())

    def at(y, p, row=LO):
        return ((y * planes + p) + SPARE) * ROWS + row

    def lines(y, n=1):
        return pl.ds(y * planes + SPARE, n * planes)

    def spot(y):
        return SEG + y * planes

    low, high = DEEP, across + DEEP - 1
    EDGE = {1: (high, low - 1), -1: (low, high + 1)}
    BEHIND = {1: (high - 1, low - 2), -1: (low + 1, high + 2)}
    own_pairs = list(range(DEEP, DEEP + across, 2))
    all_pairs = list(range(0, total, 2))

    def pair_of(y):
        return y - y % 2

    def along_z(load, cz):
        v = load(0)
        if cz == 1:
            return pltpu.roll(jnp.where(lane == W - 1, load(-1), v), 1, 1)
        if cz == -1:
            return pltpu.roll(jnp.where(lane == 0, load(1), v), W - 1, 1)
        return v

    def move_mask(y):
        for p in range(planes):
            for i, cz in enumerate((1, -1)):
                moved_mask[i, y, p] = along_z(lambda o: mask[pl.ds(at(y, p, LO + o), SEG), :], cz)

    def streamed(step, p, y, ks=range(19)):
        f = {}
        for k in ks:
            cx, cy, cz = velocities[k]
            here = state[step][SLOT[opposite[k]], pl.ds(at(y, p), SEG), :]
            q = p - cx
            if k == 0 or not 0 <= q < planes:
                f[k] = here
                continue
            moved = along_z(lambda o: state[step][SLOT[k], pl.ds(at(y - cy, q, LO + o), SEG), :], cz)
            blocked = mask[pl.ds(at(y - cy, q), SEG), :] if cz == 0 else moved_mask[(1 - cz) // 2, y - cy, q]
            f[k] = jnp.where(blocked != 0, here, moved)
        return f

    def relax(step, f, p, y, ks=range(19)):
        out = collide(f, force)
        for k in ks:
            state[step][SLOT[k], pl.ds(at(y, p), SEG), :] = out[k]

    def advance(step, y):
        for p in range(planes):
            relax(step, streamed(step - 1, p, y), p, y)

    def final(y):
        for p in range(planes):
            rho, jx, jy, jz = moments(streamed(STEPS - 1, p, y))[-4:]
            fluid = (1 - mask[pl.ds(at(y, p), SEG), :]).astype(jnp.float32)
            scale = fluid * (1.0 / reference_mach) / rho
            rows = pl.ds(y - DEEP, SEG, stride=across)
            out_ref[0, p, rows, :] = rho * fluid
            out_ref[1, p, rows, :] = jx * scale
            out_ref[2, p, rows, :] = jy * scale
            out_ref[3, p, rows, :] = jz * scale

    def strip_rows(y):
        return pl.ds(spot(y), SEG)

    def every_line(y, row):
        return pl.ds(at(y, 0, row), SEG, stride=ROWS)

    def strip_move(ref_strip, ref_lines, y, c):
        cx, cy, cz = c
        v = ref_strip(strip_rows(y - cy))
        if cz == 1:
            v = pltpu.roll(jnp.where(lane == W - 1, ref_lines(every_line(y - cy, HI - 1)), v), 1, 1)
        elif cz == -1:
            v = pltpu.roll(jnp.where(lane == 0, ref_lines(every_line(y - cy, LO)), v), W - 1, 1)
        return pltpu.roll(v, cx % SEG, 0) if cx else v

    def flag_strip(y, ks=range(19)):
        for k in ks:
            cx = velocities[k][0]
            if k == 0:
                continue
            v = strip_move(lambda rows: strip_mask[rows, :], lambda rows: mask[rows, :], y, velocities[k])
            if cx:
                v = jnp.where(plane_of == (0 if cx == 1 else planes - 1), 1, v)
            strip_flag[k, y] = v

    def strip_streamed(step, y, ks=range(19)):
        f = {}
        for k in ks:
            slot = SLOT[k]
            here = strips[step][SLOT[opposite[k]], strip_rows(y), :]
            if k == 0:
                f[k] = here
                continue
            moved = strip_move(
                lambda rows: strips[step][slot, rows, :], lambda rows: state[step][slot, rows, :], y, velocities[k]
            )
            f[k] = jnp.where(strip_flag[k, y] != 0, here, moved)
        return f

    def attach(ref, k, y, value):
        cz = velocities[k][2]
        if cz:
            ref[SLOT[k], every_line(y, LO - 1 if cz == 1 else HI), :] = value

    def strip_relax(step, f, y):
        out = collide(f, force)
        for k in range(19):
            if step < STEPS - 1:
                strips[step][SLOT[k], strip_rows(y), :] = out[k]
            attach(state[step], k, y, out[k])

    def strip_advance(step, y):
        strip_relax(step, strip_streamed(step - 1, y), y)

    load_mask.wait()
    for p in range(planes):
        for y in range(across):
            mask[pl.ds(at(y + DEEP, p), SEG), :] = raw_mask[p, pl.ds(y, SEG, stride=across), :]
    load_force.wait()
    force = [(force_ref[i] * (1.0 / 12.0), force_ref[i] * 0.1875) for i in range(3)]
    group = max(u for u in (4, 2, 1) if across % u == 0)
    for p in range(planes):
        load_pop[p].wait()

        def first(i, carry, p=p):
            for n in range(group):
                y = i * group + n
                f = [raw[k, p, pl.ds(y, SEG, stride=across), :] for k in range(19)]
                base = pl.multiple_of(at(y + DEEP, p), 8)
                for k, value in enumerate(collide(f, force)):
                    state[0][SLOT[k], pl.ds(base, SEG), :] = value
            return carry

        lax.fori_loop(0, across // group, first, 0)

    groups = [(y, k) for y in own_pairs for k in range(19)]
    per_tile = W // STRIP

    def pack(out, tile, i, loads):
        row = HI - 1 if i == 0 else LO
        packed = jnp.zeros((SEG, W), out.dtype)
        for j, load in enumerate(loads):
            shift = (STRIP * j + (STRIP if i == 0 else 0)) % W
            v = load(row)
            packed = jnp.where(triple == j, pltpu.roll(v, shift, 1) if shift else v, packed)
        out[i, tile] = packed

    def unpack(into, tile, j):
        left, right = into[0, tile], into[1, tile]
        a, b = (W - STRIP - STRIP * j) % W, (W - STRIP * j) % W
        left = pltpu.roll(left, a, 1) if a else left
        right = pltpu.roll(right, b, 1) if b else right
        return jnp.where(lane < W // 2, right, left)

    tiles = [groups[n : n + per_tile] for n in range(0, len(groups), per_tile)]
    for i in range(2):
        pack(mzs, 0, i, [lambda row, y=y: mask[every_line(y, row), :] for y in own_pairs])
        for t, tile in enumerate(tiles):
            pack(zs, t, i, [lambda row, y=y, k=k: state[0][SLOT[k], every_line(y, row), :] for y, k in tile])

    pl.semaphore_wait(barrier, len(SIDES))
    coming_z = []
    for i, dz in enumerate((1, -1)):
        coming_z.append(send(mzs.at[i], mzh.at[i], (0, dz)))
        coming_z.append(send(zs.at[i], zh.at[i], (0, dz)))
    coming_mask, coming1, coming2, coming3 = [], [], [], []
    for dy in (1, -1):
        here, there = min(EDGE[dy][0], BEHIND[dy][0]), min(EDGE[dy][1], BEHIND[dy][1])
        coming_mask.append(send(mask_view.at[lines(here, 2), line], mask_view.at[lines(there, 2), line], (dy, 0)))
    for dy in (1, -1):
        (here, there), run = EDGE[dy], pl.ds(*Y_RUN[dy])
        coming1.append(send(views[0].at[run, lines(here), line], views[0].at[run, lines(there), line], (dy, 0)))

    arrive(coming_z)
    for j, y in enumerate(own_pairs):
        value = unpack(mzh, 0, j)
        strip_mask[strip_rows(y), :] = value
        mask[every_line(y, LO - 1), :] = value
        mask[every_line(y, HI), :] = value
    for t, tile in enumerate(tiles):
        for j, (y, k) in enumerate(tile):
            value = unpack(zh, t, j)
            strip0[SLOT[k], strip_rows(y), :] = value
            attach(cells0, k, y, value)
    for y in range(low, high + 1):
        move_mask(y)
    for dy in (1, -1):
        flag_strip(pair_of(EDGE[dy][0]), PART[dy])

    def half(dy):
        return (slice(planes, 2 * planes), slice(0, planes)) if dy == 1 else (slice(0, planes), slice(planes, 2 * planes))

    for i, dy in enumerate((1, -1)):
        here, there = EDGE[dy]
        run = pl.ds(*Y_RUN[dy])
        for p in range(planes):
            f = streamed(0, p, here, PART[dy])
            for n, k in enumerate(PART[dy]):
                part[i, n, p] = f[k]
        coming2.append(send(part.at[i], part_h.at[i], (dy, 0)))
    for i, dy in enumerate((1, -1)):
        here, there = EDGE[dy]
        run = pl.ds(*Y_RUN[dy])
        f = strip_streamed(0, pair_of(here), PART[dy])
        for n, k in enumerate(PART[dy]):
            spart[i, n] = f[k]
        coming2.append(send(spart.at[i, :, half(dy)[0]], spart_h.at[i, :, half(dy)[0]], (dy, 0)))
        coming1.append(send(strip0.at[run, pl.ds(spot(here), planes)], strip0.at[run, pl.ds(spot(there), planes)], (dy, 0)))
        a, b = pair_of(here), pair_of(there)
        coming_mask.append(send(strip_mask.at[strip_rows(a)], strip_mask.at[strip_rows(b)], (dy, 0)))
    for i, dy in enumerate((1, -1)):
        here, there = BEHIND[dy]
        run = pl.ds(*Y_RUN[dy])
        advance(1, here)
        coming3.append(send(views[1].at[run, lines(here), line], views[1].at[run, lines(there), line], (dy, 0)))
    for y in range(low + 1, high, 2):
        flag_strip(y)
        strip_advance(1, y)
    for i, dy in enumerate((1, -1)):
        here, there = BEHIND[dy]
        for n, k in enumerate(Y_SET[dy]):
            third[i, n] = strip1[SLOT[k], strip_rows(pair_of(here)), :]
        coming3.append(send(third.at[i, :, half(dy)[1]], third_h.at[i, :, half(dy)[1]], (dy, 0)))

    def over(first_row, last_row, block):
        def body(y, carry):
            block(y)
            return carry

        lax.fori_loop(first_row, last_row + 1, body, 0)

    over(low + 2, high - 2, functools.partial(advance, 1))
    over(low + 2, high - 2, functools.partial(advance, 2))
    for y in own_pairs[1:-1]:
        flag_strip(y)
        strip_advance(2, y)
    over(low + 3, high - 3, final)

    arrive(coming_mask)
    for dy in (1, -1):
        y = pair_of(EDGE[dy][1])
        value = strip_mask[strip_rows(y), :]
        mask[every_line(y, LO - 1), :] = value
        mask[every_line(y, HI), :] = value
        for there in (EDGE[dy][1], BEHIND[dy][1]):
            move_mask(there)
    for y in all_pairs:
        if y not in own_pairs[1:-1]:
            flag_strip(y)
    arrive(coming1)
    for dy in (1, -1):
        y = pair_of(EDGE[dy][1])
        for k in Y_SET[dy]:
            attach(cells0, k, y, strip0[SLOT[k], strip_rows(y), :])

    def finish(halves, i, dy, y):
        for p in range(planes):
            f = streamed(0, p, y, Y_SET[-dy])
            f.update({k: halves[i, n, p] for n, k in enumerate(PART[dy])})
            relax(1, f, p, y)

    for i, dy in enumerate((1, -1)):
        finish(part, i, dy, EDGE[dy][0])
        strip_advance(1, pair_of(EDGE[dy][0]))
    for dy in (1, -1):
        advance(2, BEHIND[dy][0])

    arrive(coming2)
    for i, dy in enumerate((1, -1)):
        y = EDGE[dy][1]
        finish(part_h, i, dy, y)
        y = pair_of(y)
        f = strip_streamed(0, y, Y_SET[-dy])
        f.update({k: spart_h[i, n] for n, k in enumerate(PART[dy])})
        strip_relax(1, f, y)
    for dy in (1, -1):
        advance(2, EDGE[dy][0])
        strip_advance(2, pair_of(EDGE[dy][0]))
    for y in (low + 1, low + 2, high - 2, high - 1):
        final(y)

    arrive(coming3)
    for i, dy in enumerate((1, -1)):
        y, behind = EDGE[dy][1], BEHIND[dy][1]
        pair = pair_of(y)
        for n, k in enumerate(Y_SET[dy]):
            strip1[SLOT[k], pl.ds(spot(behind), planes), :] = third_h[i, n, half(dy)[1], :]
            if velocities[k][2]:
                attach(cells1, k, pair, strip1[SLOT[k], strip_rows(pair), :])
        for p in range(planes):
            relax(2, streamed(1, p, y), p, y, Y_SET[dy])
        strip_advance(2, pair)
        final(low if dy == 1 else high)
    for copy in sent:
        copy.wait_send()


def hand_out(both_ref, den_hbm, vel_hbm, sem):
    den = pltpu.make_async_copy(both_ref.at[0], den_hbm, sem.at[0])
    vel = pltpu.make_async_copy(both_ref.at[pl.ds(1, 3)], vel_hbm, sem.at[1])
    vel.start()
    den.start()
    vel.wait()
    den.wait()


def solution(mesh):
    gy, gz = mesh.shape["gy"], mesh.shape["gz"]

    def tiles(x, across):
        lead = x.shape[:-2]
        x = x.reshape(*lead, across, SEG, W)
        return jnp.swapaxes(x, -3, -2).reshape(*lead, SEG * across, W)

    def lines(x, across):
        lead = x.shape[:-2]
        x = x.reshape(*lead, SEG, across, W)
        return jnp.swapaxes(x, -3, -2).reshape(*lead, across, SEG * W)

    def local(populations, solid_mask, body_force):
        planes, across, length = solid_mask.shape
        if length != SEG * W or across < 8 or across % 2 or 2 * planes != SEG:
            raise ValueError("unsupported block")
        messages = 32
        total = across + 2 * DEEP
        entries = (total * planes + 2 * SPARE) * ROWS
        strip = total * planes + 2 * SEG
        packs = -(-19 * (across // 2) // (W // STRIP))
        both = pl.pallas_call(
            functools.partial(kernel, gy, gz),
            out_shape=pltpu.VMEM((4, planes, SEG * across, W), jnp.float32),
            in_specs=[pl.BlockSpec(memory_space=pltpu.HBM)] * 3,
            out_specs=pl.BlockSpec(memory_space=pltpu.VMEM),
            scratch_shapes=[
                pltpu.VMEM((19, planes, SEG * across, W), jnp.float32),
                pltpu.VMEM((planes, SEG * across, W), jnp.int32),
                pltpu.SMEM((3,), jnp.float32),
                *[pltpu.VMEM((19, entries, W), jnp.float32)] * STEPS,
                *[pltpu.VMEM((19, strip, W), jnp.float32)] * (STEPS - 1),
                pltpu.VMEM((entries, W), jnp.int32),
                pltpu.VMEM((2, total, planes, SEG, W), jnp.int32),
                pltpu.VMEM((strip, W), jnp.int32),
                pltpu.VMEM((19, total, SEG, W), jnp.int32),
                *[pltpu.VMEM((2, packs, SEG, W), jnp.float32)] * 2,
                *[pltpu.VMEM((2, 1, SEG, W), jnp.int32)] * 2,
                *[pltpu.VMEM((2, 14, planes, SEG, W), jnp.float32)] * 2,
                *[pltpu.VMEM((2, 14, SEG, W), jnp.float32)] * 2,
                *[pltpu.VMEM((2, 5, SEG, W), jnp.float32)] * 2,
                pltpu.SemaphoreType.DMA((2 + planes,)),
                pltpu.SemaphoreType.DMA((messages,)),
                pltpu.SemaphoreType.DMA((messages,)),
            ],
            compiler_params=pltpu.CompilerParams(collective_id=0, has_side_effects=True, vmem_limit_bytes=VMEM_LIMIT),
        )(*[pltpu.with_memory_space_constraint(x, pltpu.HBM) for x in (tiles(populations, across), tiles(solid_mask, across), body_force)])
        density, velocity = pl.pallas_call(
            hand_out,
            out_shape=(
                jax.ShapeDtypeStruct((planes, SEG * across, W), jnp.float32),
                jax.ShapeDtypeStruct((3, planes, SEG * across, W), jnp.float32),
            ),
            in_specs=[pl.BlockSpec(memory_space=pltpu.VMEM)],
            out_specs=(pl.BlockSpec(memory_space=pl.ANY), pl.BlockSpec(memory_space=pl.ANY)),
            scratch_shapes=[pltpu.SemaphoreType.DMA((2,))],
            compiler_params=pltpu.CompilerParams(vmem_limit_bytes=1 << 20),
        )(both)
        return lines(density, across), lines(velocity, across)

    return jax.shard_map(
        local,
        mesh=mesh,
        in_specs=(P(None, None, "gy", "gz"), P(None, "gy", "gz"), P()),
        out_specs=(P(None, "gy", "gz"), P(None, None, "gy", "gz")),
        check_vma=False,
    )
```

time: 27.7 us -> 21.2 us (0.77)
  the two profiles are of different devices: /device:TPU:0 before, /device:TPU:1 now
where the time goes in v4:
time: 21.2 us; the launch traced here: 21.1 us
  Pallas kernels  20.4 us (96%)
  between operations  0.64 us (3%)
    pallas_call x1, Pallas kernels, local(): pl.pallas_call(functools.partial(kernel, gy, gz), out_shape=pltpu.VMEM((4...  19.6 us
    pallas_call x1, Pallas kernels, local(): pl.pallas_call(hand_out, out_shape=(jax.ShapeDtypeStruct((planes, SEG * a...  0.8 us

profile of v4, /device:TPU:1, one launch (start us, length us, event | category | flops | bytes accessed | tf_op | source)
XLA Modules:
  0.0 21.1 jit_solution(15710978424902086373)
XLA Ops:
  0.6 19.6 %shard_map.50.both_ref = f32[4,4,64,128]{3,2,1,0:T(8,128)S(1)} custom-call(f32[19,4,64,128]{3,2,1,0:T(8,128)} %bitcast.20, s32[4,64,128]{2,1,0:T(8,128)} %bitcast.21, f32[3]{0:T(128)} %force_hbm.1), custom_call_target="tpu_custom_call" | custom-call | tf_op jit(solution)/shard_map/pallas_call | solution.py:480
  20.3 0.8 %shard_map.51 = (f32[4,64,128]{2,1,0:T(8,128)}, f32[3,4,64,128]{3,2,1,0:T(8,128)}) custom-call(f32[4,4,64,128]{3,2,1,0:T(8,128)S(1)} %shard_map.50.both_ref), custom_call_target="tpu_custom_call" | custom-call | tf_op jit(solution)/shard_map/pallas_call | solution.py:506

commit v5 on v4

--- a/solution.py
+++ b/solution.py
@@ -92,7 +92,8 @@
 
 
 def kernel(gy, gz, pop_hbm, mask_hbm, force_hbm, out_ref, raw, raw_mask, force_ref, cells0, cells1, cells2, strip0, strip1,
-           mask, moved_mask, strip_mask, strip_flag, zs, zh, mzs, mzh, part, part_h, spart, spart_h, third, third_h,
+           mask, moved_mask, strip_mask, strip_flag, zs, zh, mzs, mzh, part_e, part, part_h, third_e, spart, spart_h,
+           third, third_h,
            load_sem, send_sem, recv_sem):
     state, strips = (cells0, cells1, cells2), (strip0, strip1)
     planes, across = pop_hbm.shape[1], pop_hbm.shape[2] // SEG
@@ -269,30 +270,31 @@
             mask[pl.ds(at(y + DEEP, p), SEG), :] = raw_mask[p, pl.ds(y, SEG, stride=across), :]
     load_force.wait()
     force = [(force_ref[i] * (1.0 / 12.0), force_ref[i] * 0.1875) for i in range(3)]
-    group = max(u for u in (4, 2, 1) if across % u == 0)
+
+    def first(p, y):
+        f = [raw[k, p, pl.ds(y - DEEP, SEG, stride=across), :] for k in range(19)]
+        for k, value in enumerate(collide(f, force)):
+            state[0][SLOT[k], pl.ds(at(y, p), SEG), :] = value
+
+    def first_rows(*rows):
+        for y in rows:
+            for p in range(planes):
+                first(p, y)
+
     for p in range(planes):
         load_pop[p].wait()
-
-        def first(i, carry, p=p):
-            for n in range(group):
-                y = i * group + n
-                f = [raw[k, p, pl.ds(y, SEG, stride=across), :] for k in range(19)]
-                base = pl.multiple_of(at(y + DEEP, p), 8)
-                for k, value in enumerate(collide(f, force)):
-                    state[0][SLOT[k], pl.ds(base, SEG), :] = value
-            return carry
-
-        lax.fori_loop(0, across // group, first, 0)
-
-    groups = [(y, k) for y in own_pairs for k in range(19)]
+        first(p, low)
+        first(p, high)
+
+    groups = [(p, k) for p in range(planes) for k in range(19)]
     per_tile = W // STRIP
 
     def pack(out, tile, i, loads):
-        row = HI - 1 if i == 0 else LO
+        end = pl.ds((SEG - 1) * across, across) if i == 0 else pl.ds(0, across)
         packed = jnp.zeros((SEG, W), out.dtype)
         for j, load in enumerate(loads):
             shift = (STRIP * j + (STRIP if i == 0 else 0)) % W
-            v = load(row)
+            v = load(end)
             packed = jnp.where(triple == j, pltpu.roll(v, shift, 1) if shift else v, packed)
         out[i, tile] = packed
 
@@ -305,9 +307,9 @@
 
     tiles = [groups[n : n + per_tile] for n in range(0, len(groups), per_tile)]
     for i in range(2):
-        pack(mzs, 0, i, [lambda row, y=y: mask[every_line(y, row), :] for y in own_pairs])
+        pack(mzs, 0, i, [lambda end, p=p: raw_mask[p, end, :] for p in range(planes)])
         for t, tile in enumerate(tiles):
-            pack(zs, t, i, [lambda row, y=y, k=k: state[0][SLOT[k], every_line(y, row), :] for y, k in tile])
+            pack(zs, t, i, [lambda end, p=p, k=k: raw[k, p, end, :] for p, k in tile])
 
     pl.semaphore_wait(barrier, len(SIDES))
     coming_z = []
@@ -322,33 +324,68 @@
         (here, there), run = EDGE[dy], pl.ds(*Y_RUN[dy])
         coming1.append(send(views[0].at[run, lines(here), line], views[0].at[run, lines(there), line], (dy, 0)))
 
+    def half(dy):
+        return (slice(planes, 2 * planes), slice(0, planes)) if dy == 1 else (slice(0, planes), slice(planes, 2 * planes))
+
+    middle, ends = slice(1, SEG - 1), (slice(0, 1), slice(SEG - 1, SEG))
+
+    def shifted(rows, by=LO):
+        return slice(rows.start + by, rows.stop + by)
+
+    first_rows(low + 1, high - 1)
+    for y in (low, low + 1, high - 1, high):
+        move_mask(y)
+    for i, dy in enumerate((1, -1)):
+        for p in range(planes):
+            f = streamed(0, p, EDGE[dy][0], PART[dy])
+            for n, k in enumerate(PART[dy]):
+                part_e[i, n, p] = f[k]
+        coming2.append(send(part_e.at[i, :, :, middle], part_h.at[i, :, :, middle], (dy, 0)))
+    first_rows(low + 2, high - 2)
+    for y in (low + 2, high - 2):
+        move_mask(y)
+    for i, dy in enumerate((1, -1)):
+        here, there = BEHIND[dy]
+        run = pl.ds(*Y_RUN[dy])
+        for p in range(planes):
+            f = collide(streamed(0, p, here), force)
+            for n, k in enumerate(Y_SET[dy]):
+                third_e[i, n, p] = f[k]
+        coming3.append(send(third_e.at[i, :, :, middle], views[1].at[run, lines(there), shifted(middle)], (dy, 0)))
+
+    def rest(y, carry):
+        first_rows(y)
+        return carry
+
+    lax.fori_loop(low + 3, high - 2, rest, 0)
+
     arrive(coming_z)
-    for j, y in enumerate(own_pairs):
-        value = unpack(mzh, 0, j)
-        strip_mask[strip_rows(y), :] = value
-        mask[every_line(y, LO - 1), :] = value
-        mask[every_line(y, HI), :] = value
+
+    def every_row(p):
+        return pl.ds(spot(low) + p, SEG, stride=planes)
+
+    for p in range(planes):
+        value = unpack(mzh, 0, p)
+        strip_mask[every_row(p), :] = value
+        mask[pl.ds(at(low, p, LO - 1), SEG, stride=planes * ROWS), :] = value
+        mask[pl.ds(at(low, p, HI), SEG, stride=planes * ROWS), :] = value
     for t, tile in enumerate(tiles):
-        for j, (y, k) in enumerate(tile):
-            value = unpack(zh, t, j)
-            strip0[SLOT[k], strip_rows(y), :] = value
-            attach(cells0, k, y, value)
+        for j, (p, k) in enumerate(tile):
+            strip0[SLOT[k], every_row(p), :] = unpack(zh, t, j)
+    for y in own_pairs:
+        strip_relax(0, [strip0[SLOT[k], strip_rows(y), :] for k in range(19)], y)
     for y in range(low, high + 1):
         move_mask(y)
-    for dy in (1, -1):
-        flag_strip(pair_of(EDGE[dy][0]), PART[dy])
-
-    def half(dy):
-        return (slice(planes, 2 * planes), slice(0, planes)) if dy == 1 else (slice(0, planes), slice(planes, 2 * planes))
-
-    for i, dy in enumerate((1, -1)):
-        here, there = EDGE[dy]
-        run = pl.ds(*Y_RUN[dy])
-        for p in range(planes):
-            f = streamed(0, p, here, PART[dy])
+
+    for i, dy in enumerate((1, -1)):
+        for p in range(planes):
+            f = streamed(0, p, EDGE[dy][0], PART[dy])
             for n, k in enumerate(PART[dy]):
                 part[i, n, p] = f[k]
-        coming2.append(send(part.at[i], part_h.at[i], (dy, 0)))
+        for rows in ends:
+            coming2.append(send(part.at[i, :, :, rows], part_h.at[i, :, :, rows], (dy, 0)))
+    for dy in (1, -1):
+        flag_strip(pair_of(EDGE[dy][0]), PART[dy])
     for i, dy in enumerate((1, -1)):
         here, there = EDGE[dy]
         run = pl.ds(*Y_RUN[dy])
@@ -363,7 +400,9 @@
         here, there = BEHIND[dy]
         run = pl.ds(*Y_RUN[dy])
         advance(1, here)
-        coming3.append(send(views[1].at[run, lines(here), line], views[1].at[run, lines(there), line], (dy, 0)))
+        for rows in ends:
+            rows = shifted(rows)
+            coming3.append(send(views[1].at[run, lines(here), rows], views[1].at[run, lines(there), rows], (dy, 0)))
     for y in range(low + 1, high, 2):
         flag_strip(y)
         strip_advance(1, y)
@@ -470,13 +509,13 @@
 
     def local(populations, solid_mask, body_force):
         planes, across, length = solid_mask.shape
-        if length != SEG * W or across < 8 or across % 2 or 2 * planes != SEG:
+        if length != SEG * W or across != SEG or 2 * planes != SEG:
             raise ValueError("unsupported block")
-        messages = 32
+        messages = 48
         total = across + 2 * DEEP
         entries = (total * planes + 2 * SPARE) * ROWS
         strip = total * planes + 2 * SEG
-        packs = -(-19 * (across // 2) // (W // STRIP))
+        packs = -(-19 * planes // (W // STRIP))
         both = pl.pallas_call(
             functools.partial(kernel, gy, gz),
             out_shape=pltpu.VMEM((4, planes, SEG * across, W), jnp.float32),
@@ -494,7 +533,8 @@
                 pltpu.VMEM((19, total, SEG, W), jnp.int32),
                 *[pltpu.VMEM((2, packs, SEG, W), jnp.float32)] * 2,
                 *[pltpu.VMEM((2, 1, SEG, W), jnp.int32)] * 2,
-                *[pltpu.VMEM((2, 14, planes, SEG, W), jnp.float32)] * 2,
+                *[pltpu.VMEM((2, 14, planes, SEG, W), jnp.float32)] * 3,
+                pltpu.VMEM((2, 5, planes, SEG, W), jnp.float32),
                 *[pltpu.VMEM((2, 14, SEG, W), jnp.float32)] * 2,
                 *[pltpu.VMEM((2, 5, SEG, W), jnp.float32)] * 2,
                 pltpu.SemaphoreType.DMA((2 + planes,)),

time: 21.2 us -> 20.4 us (0.962)
  Pallas kernels: 20.4 us -> 19.6 us
    pallas_call x1, Pallas kernels: 19.6 us -> 18.8 us  [local(): pl.pallas_call(functools.partial(kernel, gy, gz), out_shape=pltpu.VMEM((4...]
where the time goes in v5:
time: 20.4 us; the launch traced here: 20.2 us
  Pallas kernels  19.6 us (96%)
  between operations  0.64 us (3%)
    pallas_call x1, Pallas kernels, local(): pl.pallas_call(functools.partial(kernel, gy, gz), out_shape=pltpu.VMEM((4...  18.8 us
    pallas_call x1, Pallas kernels, local(): pl.pallas_call(hand_out, out_shape=(jax.ShapeDtypeStruct((planes, SEG * a...  0.8 us

profile of v5, /device:TPU:1, one launch (start us, length us, event | category | flops | bytes accessed | tf_op | source)
XLA Modules:
  0.0 20.2 jit_solution(14958098341761055230)
XLA Ops:
  0.6 18.8 %shard_map.50.both_ref = f32[4,4,64,128]{3,2,1,0:T(8,128)S(1)} custom-call(f32[19,4,64,128]{3,2,1,0:T(8,128)} %bitcast.20, s32[4,64,128]{2,1,0:T(8,128)} %bitcast.21, f32[3]{0:T(128)} %force_hbm.1), custom_call_target="tpu_custom_call" | custom-call | tf_op jit(solution)/shard_map/pallas_call | solution.py:519
  19.4 0.8 %shard_map.51 = (f32[4,64,128]{2,1,0:T(8,128)}, f32[3,4,64,128]{3,2,1,0:T(8,128)}) custom-call(f32[4,4,64,128]{3,2,1,0:T(8,128)S(1)} %shard_map.50.both_ref), custom_call_target="tpu_custom_call" | custom-call | tf_op jit(solution)/shard_map/pallas_call | solution.py:546

commit v6 on v5

--- a/solution.py
+++ b/solution.py
@@ -92,7 +92,7 @@
 
 
 def kernel(gy, gz, pop_hbm, mask_hbm, force_hbm, out_ref, raw, raw_mask, force_ref, cells0, cells1, cells2, strip0, strip1,
-           mask, moved_mask, strip_mask, strip_flag, zs, zh, mzs, mzh, part_e, part, part_h, third_e, spart, spart_h,
+           mask, moved_mask, strip_mask, strip_flag, zs, zh, mzs, mzh, part_e, part, part_h, spart, spart_h,
            third, third_h,
            load_sem, send_sem, recv_sem):
     state, strips = (cells0, cells1, cells2), (strip0, strip1)
@@ -329,9 +329,6 @@
 
     middle, ends = slice(1, SEG - 1), (slice(0, 1), slice(SEG - 1, SEG))
 
-    def shifted(rows, by=LO):
-        return slice(rows.start + by, rows.stop + by)
-
     first_rows(low + 1, high - 1)
     for y in (low, low + 1, high - 1, high):
         move_mask(y)
@@ -342,17 +339,6 @@
                 part_e[i, n, p] = f[k]
         coming2.append(send(part_e.at[i, :, :, middle], part_h.at[i, :, :, middle], (dy, 0)))
     first_rows(low + 2, high - 2)
-    for y in (low + 2, high - 2):
-        move_mask(y)
-    for i, dy in enumerate((1, -1)):
-        here, there = BEHIND[dy]
-        run = pl.ds(*Y_RUN[dy])
-        for p in range(planes):
-            f = collide(streamed(0, p, here), force)
-            for n, k in enumerate(Y_SET[dy]):
-                third_e[i, n, p] = f[k]
-        coming3.append(send(third_e.at[i, :, :, middle], views[1].at[run, lines(there), shifted(middle)], (dy, 0)))
-
     def rest(y, carry):
         first_rows(y)
         return carry
@@ -377,6 +363,15 @@
     for y in range(low, high + 1):
         move_mask(y)
 
+    def side_by_side(values):
+        packed = jnp.zeros((SEG, W), jnp.float32)
+        for j, v in enumerate(values):
+            packed = jnp.where((triple >> 1) == j, pltpu.roll(v, (2 * STRIP * j + STRIP) % W, 1), packed)
+        return packed
+
+    def apart(packed, j):
+        return pltpu.roll(packed, (W - STRIP - 2 * STRIP * j) % W, 1)
+
     for i, dy in enumerate((1, -1)):
         for p in range(planes):
             f = streamed(0, p, EDGE[dy][0], PART[dy])
@@ -389,28 +384,27 @@
     for i, dy in enumerate((1, -1)):
         here, there = EDGE[dy]
         run = pl.ds(*Y_RUN[dy])
-        f = strip_streamed(0, pair_of(here), PART[dy])
-        for n, k in enumerate(PART[dy]):
-            spart[i, n] = f[k]
-        coming2.append(send(spart.at[i, :, half(dy)[0]], spart_h.at[i, :, half(dy)[0]], (dy, 0)))
-        coming1.append(send(strip0.at[run, pl.ds(spot(here), planes)], strip0.at[run, pl.ds(spot(there), planes)], (dy, 0)))
+        y = pair_of(here)
+        f = strip_streamed(0, y, PART[dy])
+        values = [strip0[SLOT[k], strip_rows(y), :] for k in Y_SET[dy]] + [f[k] for k in PART[dy]]
+        spart[i] = side_by_side(values)
+        rows = half(dy)[0]
+        coming1.append(send(spart.at[i, rows], spart_h.at[i, rows], (dy, 0)))
         a, b = pair_of(here), pair_of(there)
         coming_mask.append(send(strip_mask.at[strip_rows(a)], strip_mask.at[strip_rows(b)], (dy, 0)))
     for i, dy in enumerate((1, -1)):
         here, there = BEHIND[dy]
         run = pl.ds(*Y_RUN[dy])
         advance(1, here)
-        for rows in ends:
-            rows = shifted(rows)
-            coming3.append(send(views[1].at[run, lines(here), rows], views[1].at[run, lines(there), rows], (dy, 0)))
+        coming3.append(send(views[1].at[run, lines(here), line], views[1].at[run, lines(there), line], (dy, 0)))
     for y in range(low + 1, high, 2):
         flag_strip(y)
         strip_advance(1, y)
     for i, dy in enumerate((1, -1)):
         here, there = BEHIND[dy]
-        for n, k in enumerate(Y_SET[dy]):
-            third[i, n] = strip1[SLOT[k], strip_rows(pair_of(here)), :]
-        coming3.append(send(third.at[i, :, half(dy)[1]], third_h.at[i, :, half(dy)[1]], (dy, 0)))
+        third[i] = side_by_side([strip1[SLOT[k], strip_rows(pair_of(here)), :] for k in Y_SET[dy]])
+        rows = half(dy)[1]
+        coming3.append(send(third.at[i, rows], third_h.at[i, rows], (dy, 0)))
 
     def over(first_row, last_row, block):
         def body(y, carry):
@@ -438,10 +432,12 @@
         if y not in own_pairs[1:-1]:
             flag_strip(y)
     arrive(coming1)
-    for dy in (1, -1):
+    for i, dy in enumerate((1, -1)):
         y = pair_of(EDGE[dy][1])
-        for k in Y_SET[dy]:
-            attach(cells0, k, y, strip0[SLOT[k], strip_rows(y), :])
+        for n, k in enumerate(Y_SET[dy]):
+            value = apart(spart_h[i], n)
+            strip0[SLOT[k], strip_rows(y), :] = value
+            attach(cells0, k, y, value)
 
     def finish(halves, i, dy, y):
         for p in range(planes):
@@ -454,6 +450,10 @@
         strip_advance(1, pair_of(EDGE[dy][0]))
     for dy in (1, -1):
         advance(2, BEHIND[dy][0])
+    for y in (low + 1, high - 2):
+        strip_advance(2, y)
+    for y in (low + 2, high - 2):
+        final(y)
 
     arrive(coming2)
     for i, dy in enumerate((1, -1)):
@@ -461,12 +461,12 @@
         finish(part_h, i, dy, y)
         y = pair_of(y)
         f = strip_streamed(0, y, Y_SET[-dy])
-        f.update({k: spart_h[i, n] for n, k in enumerate(PART[dy])})
+        f.update({k: apart(spart_h[i], len(Y_SET[dy]) + n) for n, k in enumerate(PART[dy])})
         strip_relax(1, f, y)
     for dy in (1, -1):
         advance(2, EDGE[dy][0])
         strip_advance(2, pair_of(EDGE[dy][0]))
-    for y in (low + 1, low + 2, high - 2, high - 1):
+    for y in (low + 1, high - 1):
         final(y)
 
     arrive(coming3)
@@ -474,7 +474,7 @@
         y, behind = EDGE[dy][1], BEHIND[dy][1]
         pair = pair_of(y)
         for n, k in enumerate(Y_SET[dy]):
-            strip1[SLOT[k], pl.ds(spot(behind), planes), :] = third_h[i, n, half(dy)[1], :]
+            strip1[SLOT[k], pl.ds(spot(behind), planes), :] = apart(third_h[i], n)[half(dy)[1], :]
             if velocities[k][2]:
                 attach(cells1, k, pair, strip1[SLOT[k], strip_rows(pair), :])
         for p in range(planes):
@@ -534,9 +534,7 @@
                 *[pltpu.VMEM((2, packs, SEG, W), jnp.float32)] * 2,
                 *[pltpu.VMEM((2, 1, SEG, W), jnp.int32)] * 2,
                 *[pltpu.VMEM((2, 14, planes, SEG, W), jnp.float32)] * 3,
-                pltpu.VMEM((2, 5, planes, SEG, W), jnp.float32),
-                *[pltpu.VMEM((2, 14, SEG, W), jnp.float32)] * 2,
-                *[pltpu.VMEM((2, 5, SEG, W), jnp.float32)] * 2,
+                *[pltpu.VMEM((2, SEG, W), jnp.float32)] * 4,
                 pltpu.SemaphoreType.DMA((2 + planes,)),
                 pltpu.SemaphoreType.DMA((messages,)),
                 pltpu.SemaphoreType.DMA((messages,)),

time: 20.4 us -> 19.1 us (0.936)
  Pallas kernels: 19.6 us -> 18.3 us
    pallas_call x1, Pallas kernels: 18.8 us -> 17.5 us  [local(): pl.pallas_call(functools.partial(kernel, gy, gz), out_shape=pltpu.VMEM((4...]
where the time goes in v6:
time: 19.1 us; the launch traced here: 18.9 us
  Pallas kernels  18.3 us (96%)
  between operations  0.64 us (3%)
    pallas_call x1, Pallas kernels, local(): pl.pallas_call(functools.partial(kernel, gy, gz), out_shape=pltpu.VMEM((4...  17.5 us
    pallas_call x1, Pallas kernels, local(): pl.pallas_call(hand_out, out_shape=(jax.ShapeDtypeStruct((planes, SEG * a...  0.8 us

profile of v6, /device:TPU:1, one launch (start us, length us, event | category | flops | bytes accessed | tf_op | source)
XLA Modules:
  0.0 18.9 jit_solution(17707036019715552445)
XLA Ops:
  0.6 17.5 %shard_map.50.both_ref = f32[4,4,64,128]{3,2,1,0:T(8,128)S(1)} custom-call(f32[19,4,64,128]{3,2,1,0:T(8,128)} %bitcast.20, s32[4,64,128]{2,1,0:T(8,128)} %bitcast.21, f32[3]{0:T(128)} %force_hbm.1), custom_call_target="tpu_custom_call" | custom-call | tf_op jit(solution)/shard_map/pallas_call | solution.py:519
  18.1 0.8 %shard_map.51 = (f32[4,64,128]{2,1,0:T(8,128)}, f32[3,4,64,128]{3,2,1,0:T(8,128)}) custom-call(f32[4,4,64,128]{3,2,1,0:T(8,128)S(1)} %shard_map.50.both_ref), custom_call_target="tpu_custom_call" | custom-call | tf_op jit(solution)/shard_map/pallas_call | solution.py:544

commit v7 on v6

--- a/solution.py
+++ b/solution.py
@@ -44,6 +44,7 @@
 PART = {dy: [k for k in ORDER if velocities[k][1] != -dy] for dy in (1, -1)}
 SIDES = [(1, 0), (-1, 0), (0, 1), (0, -1)]
 MESH = pl.DeviceIdType.MESH
+SIDE = {1: 0, -1: 1}
 
 
 def moments(f):
@@ -316,13 +317,13 @@
     for i, dz in enumerate((1, -1)):
         coming_z.append(send(mzs.at[i], mzh.at[i], (0, dz)))
         coming_z.append(send(zs.at[i], zh.at[i], (0, dz)))
-    coming_mask, coming1, coming2, coming3 = [], [], [], []
+    coming_mask, coming1, coming2, coming3 = ({1: [], -1: []} for _ in range(4))
     for dy in (1, -1):
         here, there = min(EDGE[dy][0], BEHIND[dy][0]), min(EDGE[dy][1], BEHIND[dy][1])
-        coming_mask.append(send(mask_view.at[lines(here, 2), line], mask_view.at[lines(there, 2), line], (dy, 0)))
+        coming_mask[dy].append(send(mask_view.at[lines(here, 2), line], mask_view.at[lines(there, 2), line], (dy, 0)))
     for dy in (1, -1):
         (here, there), run = EDGE[dy], pl.ds(*Y_RUN[dy])
-        coming1.append(send(views[0].at[run, lines(here), line], views[0].at[run, lines(there), line], (dy, 0)))
+        coming1[dy].append(send(views[0].at[run, lines(here), line], views[0].at[run, lines(there), line], (dy, 0)))
 
     def half(dy):
         return (slice(planes, 2 * planes), slice(0, planes)) if dy == 1 else (slice(0, planes), slice(planes, 2 * planes))
@@ -337,7 +338,7 @@
             f = streamed(0, p, EDGE[dy][0], PART[dy])
             for n, k in enumerate(PART[dy]):
                 part_e[i, n, p] = f[k]
-        coming2.append(send(part_e.at[i, :, :, middle], part_h.at[i, :, :, middle], (dy, 0)))
+        coming2[dy].append(send(part_e.at[i, :, :, middle], part_h.at[i, :, :, middle], (dy, 0)))
     first_rows(low + 2, high - 2)
     def rest(y, carry):
         first_rows(y)
@@ -378,7 +379,7 @@
             for n, k in enumerate(PART[dy]):
                 part[i, n, p] = f[k]
         for rows in ends:
-            coming2.append(send(part.at[i, :, :, rows], part_h.at[i, :, :, rows], (dy, 0)))
+            coming2[dy].append(send(part.at[i, :, :, rows], part_h.at[i, :, :, rows], (dy, 0)))
     for dy in (1, -1):
         flag_strip(pair_of(EDGE[dy][0]), PART[dy])
     for i, dy in enumerate((1, -1)):
@@ -389,14 +390,14 @@
         values = [strip0[SLOT[k], strip_rows(y), :] for k in Y_SET[dy]] + [f[k] for k in PART[dy]]
         spart[i] = side_by_side(values)
         rows = half(dy)[0]
-        coming1.append(send(spart.at[i, rows], spart_h.at[i, rows], (dy, 0)))
+        coming1[dy].append(send(spart.at[i, rows], spart_h.at[i, rows], (dy, 0)))
         a, b = pair_of(here), pair_of(there)
-        coming_mask.append(send(strip_mask.at[strip_rows(a)], strip_mask.at[strip_rows(b)], (dy, 0)))
+        coming_mask[dy].append(send(strip_mask.at[strip_rows(a)], strip_mask.at[strip_rows(b)], (dy, 0)))
     for i, dy in enumerate((1, -1)):
         here, there = BEHIND[dy]
         run = pl.ds(*Y_RUN[dy])
         advance(1, here)
-        coming3.append(send(views[1].at[run, lines(here), line], views[1].at[run, lines(there), line], (dy, 0)))
+        coming3[dy].append(send(views[1].at[run, lines(here), line], views[1].at[run, lines(there), line], (dy, 0)))
     for y in range(low + 1, high, 2):
         flag_strip(y)
         strip_advance(1, y)
@@ -404,7 +405,7 @@
         here, there = BEHIND[dy]
         third[i] = side_by_side([strip1[SLOT[k], strip_rows(pair_of(here)), :] for k in Y_SET[dy]])
         rows = half(dy)[1]
-        coming3.append(send(third.at[i, rows], third_h.at[i, rows], (dy, 0)))
+        coming3[dy].append(send(third.at[i, rows], third_h.at[i, rows], (dy, 0)))
 
     def over(first_row, last_row, block):
         def body(y, carry):
@@ -420,67 +421,66 @@
         strip_advance(2, y)
     over(low + 3, high - 3, final)
 
-    arrive(coming_mask)
-    for dy in (1, -1):
-        y = pair_of(EDGE[dy][1])
-        value = strip_mask[strip_rows(y), :]
-        mask[every_line(y, LO - 1), :] = value
-        mask[every_line(y, HI), :] = value
-        for there in (EDGE[dy][1], BEHIND[dy][1]):
-            move_mask(there)
-    for y in all_pairs:
-        if y not in own_pairs[1:-1]:
-            flag_strip(y)
-    arrive(coming1)
-    for i, dy in enumerate((1, -1)):
-        y = pair_of(EDGE[dy][1])
-        for n, k in enumerate(Y_SET[dy]):
+    def finish(halves, dy, y):
+        for p in range(planes):
+            f = streamed(0, p, y, Y_SET[-dy])
+            f.update({k: halves[SIDE[dy], n, p] for n, k in enumerate(PART[dy])})
+            relax(1, f, p, y)
+
+    def close(away):
+        i = SIDE[away]
+        edge, halo = EDGE[-away][0], EDGE[away][1]
+        behind, beyond = BEHIND[-away][0], BEHIND[away][1]
+        third_row = behind - (edge - behind)
+        pair, outer = pair_of(edge), pair_of(halo)
+        arrive(coming_mask[away])
+        value = strip_mask[strip_rows(outer), :]
+        mask[every_line(outer, LO - 1), :] = value
+        mask[every_line(outer, HI), :] = value
+        move_mask(halo)
+        move_mask(beyond)
+        flag_strip(pair)
+        flag_strip(outer)
+        arrive(coming1[away])
+        for n, k in enumerate(Y_SET[away]):
             value = apart(spart_h[i], n)
-            strip0[SLOT[k], strip_rows(y), :] = value
-            attach(cells0, k, y, value)
-
-    def finish(halves, i, dy, y):
-        for p in range(planes):
-            f = streamed(0, p, y, Y_SET[-dy])
-            f.update({k: halves[i, n, p] for n, k in enumerate(PART[dy])})
-            relax(1, f, p, y)
-
-    for i, dy in enumerate((1, -1)):
-        finish(part, i, dy, EDGE[dy][0])
-        strip_advance(1, pair_of(EDGE[dy][0]))
-    for dy in (1, -1):
-        advance(2, BEHIND[dy][0])
-    for y in (low + 1, high - 2):
-        strip_advance(2, y)
-    for y in (low + 2, high - 2):
-        final(y)
-
-    arrive(coming2)
-    for i, dy in enumerate((1, -1)):
-        y = EDGE[dy][1]
-        finish(part_h, i, dy, y)
-        y = pair_of(y)
-        f = strip_streamed(0, y, Y_SET[-dy])
-        f.update({k: apart(spart_h[i], len(Y_SET[dy]) + n) for n, k in enumerate(PART[dy])})
-        strip_relax(1, f, y)
-    for dy in (1, -1):
-        advance(2, EDGE[dy][0])
-        strip_advance(2, pair_of(EDGE[dy][0]))
-    for y in (low + 1, high - 1):
-        final(y)
-
-    arrive(coming3)
-    for i, dy in enumerate((1, -1)):
-        y, behind = EDGE[dy][1], BEHIND[dy][1]
-        pair = pair_of(y)
-        for n, k in enumerate(Y_SET[dy]):
-            strip1[SLOT[k], pl.ds(spot(behind), planes), :] = apart(third_h[i], n)[half(dy)[1], :]
+            strip0[SLOT[k], strip_rows(outer), :] = value
+            attach(cells0, k, outer, value)
+        finish(part, -away, edge)
+        strip_advance(1, pair)
+        advance(2, behind)
+        strip_advance(2, min(behind, third_row))
+        final(third_row)
+        arrive(coming2[away])
+        finish(part_h, away, halo)
+        f = strip_streamed(0, outer, Y_SET[-away])
+        f.update({k: apart(spart_h[i], len(Y_SET[away]) + n) for n, k in enumerate(PART[away])})
+        strip_relax(1, f, outer)
+        advance(2, edge)
+        strip_advance(2, pair)
+        final(behind)
+        arrive(coming3[away])
+        for n, k in enumerate(Y_SET[away]):
+            strip1[SLOT[k], pl.ds(spot(beyond), planes), :] = apart(third_h[i], n)[half(away)[1], :]
             if velocities[k][2]:
-                attach(cells1, k, pair, strip1[SLOT[k], strip_rows(pair), :])
-        for p in range(planes):
-            relax(2, streamed(1, p, y), p, y, Y_SET[dy])
-        strip_advance(2, pair)
-        final(low if dy == 1 else high)
+                attach(cells1, k, outer, strip1[SLOT[k], strip_rows(outer), :])
+        for p in range(planes):
+            relax(2, streamed(1, p, halo), p, halo, Y_SET[away])
+        strip_advance(2, outer)
+        final(edge)
+
+    odd = lax.rem(my, 2) == 1
+
+    @pl.when(odd)
+    def _():
+        close(1)
+        close(-1)
+
+    @pl.when(jnp.logical_not(odd))
+    def _():
+        close(-1)
+        close(1)
+
     for copy in sent:
         copy.wait_send()
 

time: 19.1 us -> 18.3 us (0.958)
  Pallas kernels: 18.3 us -> 17.5 us
    pallas_call x1, Pallas kernels: 17.5 us -> 16.7 us  [local(): pl.pallas_call(functools.partial(kernel, gy, gz), out_shape=pltpu.VMEM((4...]
where the time goes in v7:
time: 18.3 us; the launch traced here: 18.1 us
  Pallas kernels  17.5 us (96%)
  between operations  0.64 us (3%)
    pallas_call x1, Pallas kernels, local(): pl.pallas_call(functools.partial(kernel, gy, gz), out_shape=pltpu.VMEM((4...  16.7 us
    pallas_call x1, Pallas kernels, local(): pl.pallas_call(hand_out, out_shape=(jax.ShapeDtypeStruct((planes, SEG * a...  0.8 us

profile of v7, /device:TPU:1, one launch (start us, length us, event | category | flops | bytes accessed | tf_op | source)
XLA Modules:
  0.0 18.1 jit_solution(6682541001649652698)
XLA Ops:
  0.6 16.7 %shard_map.50.both_ref = f32[4,4,64,128]{3,2,1,0:T(8,128)S(1)} custom-call(f32[19,4,64,128]{3,2,1,0:T(8,128)} %bitcast.20, s32[4,64,128]{2,1,0:T(8,128)} %bitcast.21, f32[3]{0:T(128)} %force_hbm.1), custom_call_target="tpu_custom_call" | custom-call | tf_op jit(solution)/shard_map/pallas_call | solution.py:519
  17.3 0.8 %shard_map.51 = (f32[4,64,128]{2,1,0:T(8,128)}, f32[3,4,64,128]{3,2,1,0:T(8,128)}) custom-call(f32[4,4,64,128]{3,2,1,0:T(8,128)S(1)} %shard_map.50.both_ref), custom_call_target="tpu_custom_call" | custom-call | tf_op jit(solution)/shard_map/pallas_call | solution.py:544

commit v8 on v7

--- a/solution.py
+++ b/solution.py
@@ -37,7 +37,7 @@
 ]
 opposite = [0, 2, 1, 4, 3, 6, 5, 8, 7, 10, 9, 12, 11, 14, 13, 16, 15, 18, 17]
 reference_mach = 0.05
-ORDER = [5, 11, 14, 15, 3, 7, 10, 17, 6, 12, 13, 16, 4, 8, 9, 18, 0, 1, 2]
+ORDER = [5, 11, 14, 15, 3, 17, 7, 10, 6, 12, 13, 16, 4, 18, 9, 8, 0, 1, 2]
 SLOT = [ORDER.index(k) for k in range(19)]
 Y_RUN = {1: (3, 5), -1: (11, 5)}
 Y_SET = {dy: [k for k in ORDER if velocities[k][1] == dy] for dy in (1, -1)}
@@ -397,7 +397,10 @@
         here, there = BEHIND[dy]
         run = pl.ds(*Y_RUN[dy])
         advance(1, here)
-        coming3[dy].append(send(views[1].at[run, lines(here), line], views[1].at[run, lines(there), line], (dy, 0)))
+        for n, count_k, p, count_p in ((0, 3, 0, planes), (3, 1, 0, planes - 1), (4, 1, 1, planes - 1)):
+            slots = pl.ds(Y_RUN[dy][0] + n, count_k)
+            source, target = (pl.ds(row * planes + SPARE + p, count_p) for row in (here, there))
+            coming3[dy].append(send(views[1].at[slots, source, line], views[1].at[slots, target, line], (dy, 0)))
     for y in range(low + 1, high, 2):
         flag_strip(y)
         strip_advance(1, y)
@@ -486,12 +489,12 @@
 
 
 def hand_out(both_ref, den_hbm, vel_hbm, sem):
-    den = pltpu.make_async_copy(both_ref.at[0], den_hbm, sem.at[0])
-    vel = pltpu.make_async_copy(both_ref.at[pl.ds(1, 3)], vel_hbm, sem.at[1])
-    vel.start()
-    den.start()
-    vel.wait()
-    den.wait()
+    copies = [pltpu.make_async_copy(both_ref.at[0], den_hbm, sem.at[0])]
+    copies += [pltpu.make_async_copy(both_ref.at[1 + i], vel_hbm.at[i], sem.at[1 + i]) for i in range(3)]
+    for copy in copies:
+        copy.start()
+    for copy in copies:
+        copy.wait()
 
 
 def solution(mesh):
@@ -549,7 +552,7 @@
             ),
             in_specs=[pl.BlockSpec(memory_space=pltpu.VMEM)],
             out_specs=(pl.BlockSpec(memory_space=pl.ANY), pl.BlockSpec(memory_space=pl.ANY)),
-            scratch_shapes=[pltpu.SemaphoreType.DMA((2,))],
+            scratch_shapes=[pltpu.SemaphoreType.DMA((4,))],
             compiler_params=pltpu.CompilerParams(vmem_limit_bytes=1 << 20),
         )(both)
         return lines(density, across), lines(velocity, across)

time: 18.3 us -> 18.2 us (level)
  no operation moved by 1% of the time
where the time goes in v8:
time: 18.2 us; the launch traced here: 18.1 us
  Pallas kernels  17.4 us (96%)
  between operations  0.64 us (4%)
    pallas_call x1, Pallas kernels, local(): pl.pallas_call(functools.partial(kernel, gy, gz), out_shape=pltpu.VMEM((4...  16.6 us
    pallas_call x1, Pallas kernels, local(): pl.pallas_call(hand_out, out_shape=(jax.ShapeDtypeStruct((planes, SEG * a...  0.82 us

profile of v8, /device:TPU:1, one launch (start us, length us, event | category | flops | bytes accessed | tf_op | source)
XLA Modules:
  0.0 18.1 jit_solution(4441820839760248857)
XLA Ops:
  0.6 16.6 %shard_map.50.both_ref = f32[4,4,64,128]{3,2,1,0:T(8,128)S(1)} custom-call(f32[19,4,64,128]{3,2,1,0:T(8,128)} %bitcast.20, s32[4,64,128]{2,1,0:T(8,128)} %bitcast.21, f32[3]{0:T(128)} %force_hbm.1), custom_call_target="tpu_custom_call" | custom-call | tf_op jit(solution)/shard_map/pallas_call | solution.py:522
  17.2 0.8 %shard_map.51 = (f32[4,64,128]{2,1,0:T(8,128)}, f32[3,4,64,128]{3,2,1,0:T(8,128)}) custom-call(f32[4,4,64,128]{3,2,1,0:T(8,128)S(1)} %shard_map.50.both_ref), custom_call_target="tpu_custom_call" | custom-call | tf_op jit(solution)/shard_map/pallas_call | solution.py:547
